TPU v7x, 32 devices: a 4x4x1 block of a 4x4x8 slice. The times are simulated.
32 devices in a mesh: batch: 1 (over z), z: 4 (over y), y: 4 (over x), x: 2 (over core).
Axes of the slice: x: 4, y: 4, z: 1, core: 2. Of those that a mesh axis runs over, the one named last changes fastest.
The devices are a block of a 4x4x8 slice.
Arguments:
- volume: bfloat16 [32, 128, 256, 256], P('batch', 'x', 'y', 'z')
- filter_taps: float32 [3, 3, 17], replicated
- mix_w: bfloat16 [3, 32, 32], replicated
- mix_bias: float32 [3, 32], replicated
Outputs:
- output: bfloat16 [32, 128, 256, 256], P('batch', 'x', 'y', 'z')
All inputs are finite; a program needn't handle non-finite values.
Results may differ from a plain program's by a relative error of at most 0.00526.
Values are sent between devices in bfloat16 or wider.
A program may use at most 768 MiB of HBM per device.

v0:
```python
import jax
import jax.numpy as jnp
from jax import lax
from jax.sharding import PartitionSpec as P

PASS_FORMS = ("", "cajk,ai->cijk", "ciak,aj->cijk", "cija,ak->cijk")
GRID_AXES = ("", "x", "y", "z")


def band_matrix(taps_row, out_len):
    kernel = taps_row.shape[0]
    tap_index = jnp.arange(out_len + kernel - 1)[:, None] - jnp.arange(out_len)[None, :]
    tap_hits = tap_index[:, :, None] == jnp.arange(kernel)[None, None, :]
    taps_b = taps_row.astype(jnp.bfloat16).astype(jnp.float32)
    return jnp.sum(jnp.where(tap_hits, taps_b[None, None, :], 0.0), axis=-1).astype(jnp.bfloat16)


def with_halo(local_vol, axis_name, dim_pos, halo_width, axis_count):
    dim_len = local_vol.shape[dim_pos]
    upper_planes = lax.slice_in_dim(local_vol, dim_len - halo_width, dim_len, axis=dim_pos)
    lower_planes = lax.slice_in_dim(local_vol, 0, halo_width, axis=dim_pos)
    from_below = lax.ppermute(upper_planes, axis_name, [(i, i + 1) for i in range(axis_count - 1)])
    from_above = lax.ppermute(lower_planes, axis_name, [(i + 1, i) for i in range(axis_count - 1)])
    return jnp.concatenate([from_below, local_vol, from_above], axis=dim_pos)


def solution(mesh):
    axis_counts = (0, mesh.shape["x"], mesh.shape["y"], mesh.shape["z"])

    def local_layers(volume, filter_taps, mix_w, mix_bias):
        half_width = (filter_taps.shape[2] - 1) // 2
        for layer_idx in range(filter_taps.shape[0]):
            staged = volume
            for dim_pos in (1, 2, 3):
                padded = with_halo(staged, GRID_AXES[dim_pos], dim_pos, half_width, axis_counts[dim_pos])
                band_mat = band_matrix(filter_taps[layer_idx, dim_pos - 1], staged.shape[dim_pos])
                staged = jnp.einsum(PASS_FORMS[dim_pos], padded, band_mat, preferred_element_type=jnp.float32).astype(jnp.bfloat16)
            mixed_out = jnp.einsum("cd,cijk->dijk", mix_w[layer_idx], staged, preferred_element_type=jnp.float32)
            activated = jax.nn.gelu(mixed_out + mix_bias[layer_idx][:, None, None, None], approximate=False)
            volume = (volume.astype(jnp.float32) + activated).astype(jnp.bfloat16)
        return volume

    vol_spec = P("batch", "x", "y", "z")
    return jax.shard_map(local_layers, mesh=mesh, in_specs=(vol_spec, P(), P(), P()), out_specs=vol_spec, check_vma=False)
```

profile of v0, /device:TPU:98, one launch (start us, length us, event | category | flops | bytes accessed | tf_op | source)
XLA Modules:
  0.0 2018.7 jit_solution(10603109344257779670)
XLA Ops:
  12.5 47.0 %copy.33 = bf16[32,64,64,64]{1,3,2,0:T(8,128)(2,1)} copy(bf16[32,64,64,64]{3,2,1,0:T(8,128)(2,1)} %param.4) | data formatting | bytes 33554432 | tf_op args[0]
  111.0 51.2 %convert_bitcast_fusion.5 = bf16[32,64,64,64]{3,1,2,0:T(8,128)(2,1)} fusion(bf16[32,8,64,64]{1,3,2,0:T(8,128)(2,1)} %copy.34, bf16[32,64,64,64]{1,3,2,0:T(8,128)(2,1)} %copy.33, bf16[32,8,64,64]{1,3,2,0:T(8,128)(2,1)} %copy.32, bf16[80,64]{0,1:T(8,128)(2,1)S(1)} %get-tuple-element.12), kind=kOutput, calls=%fused_computation.110 | convolution fusion | flops 1413480448 | bytes 37758976 | tf_op jit(solution)/shard_map/cajk,ai->cijk/dot_general | solution.py:37
  175.0 84.9 %collective-permute-done.2 = bf16[32,64,8,64]{3,1,2,0:T(8,128)(2,1)} collective-permute-done((bf16[32,64,8,64]{3,1,2,0:T(8,128)(2,1)S(1)}, bf16[32,64,8,64]{3,1,2,0:T(8,128)(2,1)}, u32[]{:S(2)}, u32[]{:S(2)}) %collective-permute-start.2) | collective-permute-done | bytes 2097184 | tf_op jit(solution)/shard_map/ppermute | solution.py:22
  263.8 28.7 %pad_maximum_fusion = bf16[32,64,80,64]{3,1,2,0:T(8,128)(2,1)} fusion(bf16[32,64,8,64]{3,1,2,0:T(8,128)(2,1)} %collective-permute-done.3, bf16[32,64,64,64]{3,1,2,0:T(8,128)(2,1)} %convert_bitcast_fusion.5, bf16[32,64,8,64]{3,1,2,0:T(8,128)(2,1)} %collective-permute-done.2), kind=kLoop, calls=%fused_computation.75 | loop fusion | flops 20971520 | bytes 41943040 | tf_op jit(solution)/shard_map/concatenate | solution.py:24
  292.5 32.2 %convert_bitcast_fusion.4 = bf16[32,64,64,64]{2,3,1,0:T(8,128)(2,1)} fusion(bf16[32,64,80,64]{3,1,2,0:T(8,128)(2,1)} %pad_maximum_fusion, bf16[80,64]{0,1:T(8,128)(2,1)S(1)} %get-tuple-element.13), kind=kOutput, calls=%fused_computation.109 | convolution fusion | flops 1350565888 | bytes 37758976 | tf_op jit(solution)/shard_map/ciak,aj->cijk/dot_general | solution.py:37
  336.8 86.2 %collective-permute-done.4 = bf16[32,64,64,8]{2,3,1,0:T(8,128)(2,1)} collective-permute-done((bf16[32,64,64,8]{2,3,1,0:T(8,128)(2,1)S(1)}, bf16[32,64,64,8]{2,3,1,0:T(8,128)(2,1)}, u32[]{:S(2)}, u32[]{:S(2)}) %collective-permute-start.4) | collective-permute-done | bytes 2097184 | tf_op jit(solution)/shard_map/ppermute | solution.py:22
  458.0 47.9 %copy.36 = bf16[32,64,64,80]{3,0,2,1:T(8,128)(2,1)} copy(bf16[32,64,64,80]{2,3,1,0:T(8,128)(2,1)} %pad_maximum_fusion.1) | data formatting | bytes 41943040 | tf_op jit(solution)/shard_map/concatenate | solution.py:24
  532.0 169.9 %fusion.3 = bf16[32,64,64,64]{3,0,2,1:T(8,128)(2,1)S(1)} fusion(bf16[32,64,64,64]{3,2,1,0:T(8,128)(2,1)} %param.4, f32[32]{0:T(128)S(1)} %get-tuple-element.42, bf16[3,32,32]{2,1,0:T(8,128)(2,1)} %param.6, bf16[32,64,64,64]{3,0,2,1:T(8,128)(2,1)} %fusion.78.clone.5), kind=kOutput, calls=%fused_computation.6 | convolution fusion | flops 1107296256 | bytes 83894400 | tf_op jit(solution)/shard_map/cd,cijk->dijk/dot_general | solution.py:38
  730.9 29.0 %pad_maximum_fusion.2 = bf16[32,80,64,64]{3,0,2,1:T(8,128)(2,1)} fusion(bf16[32,8,64,64]{3,0,2,1:T(8,128)(2,1)} %collective-permute-done.7, bf16[32,64,64,64]{3,0,2,1:T(8,128)(2,1)} %copy-done.1, bf16[32,8,64,64]{3,0,2,1:T(8,128)(2,1)} %collective-permute-done.6), kind=kLoop, calls=%fused_computation.77 | loop fusion | flops 20971520 | bytes 41943040 | tf_op jit(solution)/shard_map/concatenate | solution.py:24
  759.9 57.1 %convert_bitcast_fusion.3 = bf16[32,64,64,64]{3,1,2,0:T(8,128)(2,1)} fusion(bf16[32,80,64,64]{3,0,2,1:T(8,128)(2,1)} %pad_maximum_fusion.2, bf16[80,64]{0,1:T(8,128)(2,1)S(1)} %copy-done.7), kind=kOutput, calls=%fused_computation.106 | convolution fusion | flops 1350565888 | bytes 37758976 | tf_op jit(solution)/shard_map/cajk,ai->cijk/dot_general | solution.py:37
  830.0 86.1 %collective-permute-done.8 = bf16[32,64,8,64]{3,1,2,0:T(8,128)(2,1)} collective-permute-done((bf16[32,64,8,64]{3,1,2,0:T(8,128)(2,1)S(1)}, bf16[32,64,8,64]{3,1,2,0:T(8,128)(2,1)}, u32[]{:S(2)}, u32[]{:S(2)}) %collective-permute-start.8) | collective-permute-done | bytes 2097184 | tf_op jit(solution)/shard_map/ppermute | solution.py:22
  919.3 28.7 %pad_maximum_fusion.3 = bf16[32,64,80,64]{3,1,2,0:T(8,128)(2,1)} fusion(bf16[32,64,8,64]{3,1,2,0:T(8,128)(2,1)} %collective-permute-done.9, bf16[32,64,64,64]{3,1,2,0:T(8,128)(2,1)} %convert_bitcast_fusion.3, bf16[32,64,8,64]{3,1,2,0:T(8,128)(2,1)} %collective-permute-done.8), kind=kLoop, calls=%fused_computation.78 | loop fusion | flops 20971520 | bytes 41943040 | tf_op jit(solution)/shard_map/concatenate | solution.py:24
  948.0 32.1 %convert_bitcast_fusion.2 = bf16[32,64,64,64]{2,3,1,0:T(8,128)(2,1)} fusion(bf16[32,64,80,64]{3,1,2,0:T(8,128)(2,1)} %pad_maximum_fusion.3, bf16[80,64]{0,1:T(8,128)(2,1)S(1)} %copy-done.6), kind=kOutput, calls=%fused_computation.105 | convolution fusion | flops 1350565888 | bytes 37758976 | tf_op jit(solution)/shard_map/ciak,aj->cijk/dot_general | solution.py:37
  989.7 85.7 %collective-permute-done.10 = bf16[32,64,64,8]{2,3,1,0:T(8,128)(2,1)} collective-permute-done((bf16[32,64,64,8]{2,3,1,0:T(8,128)(2,1)S(1)}, bf16[32,64,64,8]{2,3,1,0:T(8,128)(2,1)}, u32[]{:S(2)}, u32[]{:S(2)}) %collective-permute-start.10) | collective-permute-done | bytes 2097184 | tf_op jit(solution)/shard_map/ppermute | solution.py:22
  1110.0 48.0 %copy.40 = bf16[32,64,64,80]{3,0,2,1:T(8,128)(2,1)} copy(bf16[32,64,64,80]{2,3,1,0:T(8,128)(2,1)} %pad_maximum_fusion.4) | data formatting | bytes 41943040 | tf_op jit(solution)/shard_map/concatenate | solution.py:24
  1184.1 164.2 %fusion.7 = bf16[32,64,64,64]{3,0,2,1:T(8,128)(2,1)S(1)} fusion(bf16[32,64,64,64]{3,0,2,1:T(8,128)(2,1)} %copy-done.1, f32[32]{0:T(128)S(1)} %copy-done.12, bf16[3,32,32]{2,1,0:T(8,128)(2,1)} %param.6, bf16[32,64,64,64]{3,0,2,1:T(8,128)(2,1)} %fusion.76.clone.5), kind=kOutput, calls=%fused_computation.10 | convolution fusion | flops 1107296256 | bytes 83894400 | tf_op jit(solution)/shard_map/cd,cijk->dijk/dot_general | solution.py:38
  1376.4 29.0 %pad_maximum_fusion.5 = bf16[32,80,64,64]{3,0,2,1:T(8,128)(2,1)} fusion(bf16[32,8,64,64]{3,0,2,1:T(8,128)(2,1)} %collective-permute-done.13, bf16[32,64,64,64]{3,0,2,1:T(8,128)(2,1)} %copy-done, bf16[32,8,64,64]{3,0,2,1:T(8,128)(2,1)} %collective-permute-done.12), kind=kLoop, calls=%fused_computation.80 | loop fusion | flops 20971520 | bytes 41943040 | tf_op jit(solution)/shard_map/concatenate | solution.py:24
  1405.4 57.1 %convert_bitcast_fusion.1 = bf16[32,64,64,64]{3,1,2,0:T(8,128)(2,1)} fusion(bf16[32,80,64,64]{3,0,2,1:T(8,128)(2,1)} %pad_maximum_fusion.5, bf16[80,64]{0,1:T(8,128)(2,1)S(1)} %copy-done.4), kind=kOutput, calls=%fused_computation.102 | convolution fusion | flops 1350565888 | bytes 37758976 | tf_op jit(solution)/shard_map/cajk,ai->cijk/dot_general | solution.py:37
  1475.1 86.6 %collective-permute-done.14 = bf16[32,64,8,64]{3,1,2,0:T(8,128)(2,1)} collective-permute-done((bf16[32,64,8,64]{3,1,2,0:T(8,128)(2,1)S(1)}, bf16[32,64,8,64]{3,1,2,0:T(8,128)(2,1)}, u32[]{:S(2)}, u32[]{:S(2)}) %collective-permute-start.14) | collective-permute-done | bytes 2097184 | tf_op jit(solution)/shard_map/ppermute | solution.py:22
  1565.0 28.7 %pad_maximum_fusion.6 = bf16[32,64,80,64]{3,1,2,0:T(8,128)(2,1)} fusion(bf16[32,64,8,64]{3,1,2,0:T(8,128)(2,1)} %collective-permute-done.15, bf16[32,64,64,64]{3,1,2,0:T(8,128)(2,1)} %convert_bitcast_fusion.1, bf16[32,64,8,64]{3,1,2,0:T(8,128)(2,1)} %collective-permute-done.14), kind=kLoop, calls=%fused_computation.81 | loop fusion | flops 20971520 | bytes 41943040 | tf_op jit(solution)/shard_map/concatenate | solution.py:24
  1593.7 32.1 %convert_bitcast_fusion = bf16[32,64,64,64]{2,3,1,0:T(8,128)(2,1)} fusion(bf16[32,64,80,64]{3,1,2,0:T(8,128)(2,1)} %pad_maximum_fusion.6, bf16[80,64]{0,1:T(8,128)(2,1)S(1)} %copy-done.3), kind=kOutput, calls=%fused_computation.101 | convolution fusion | flops 1350565888 | bytes 37758976 | tf_op jit(solution)/shard_map/ciak,aj->cijk/dot_general | solution.py:37
  1635.0 85.9 %collective-permute-done.16 = bf16[32,64,64,8]{2,3,1,0:T(8,128)(2,1)} collective-permute-done((bf16[32,64,64,8]{2,3,1,0:T(8,128)(2,1)S(1)}, bf16[32,64,64,8]{2,3,1,0:T(8,128)(2,1)}, u32[]{:S(2)}, u32[]{:S(2)}) %collective-permute-start.16) | collective-permute-done | bytes 2097184 | tf_op jit(solution)/shard_map/ppermute | solution.py:22
  1755.6 48.0 %copy.44 = bf16[32,64,64,80]{3,0,2,1:T(8,128)(2,1)} copy(bf16[32,64,64,80]{2,3,1,0:T(8,128)(2,1)} %pad_maximum_fusion.7) | data formatting | bytes 41943040 | tf_op jit(solution)/shard_map/concatenate | solution.py:24
  1829.7 165.4 %fusion.11 = bf16[32,64,64,64]{3,0,2,1:T(8,128)(2,1)} fusion(bf16[32,64,64,64]{3,0,2,1:T(8,128)(2,1)} %copy-done, f32[32]{0:T(128)S(1)} %copy-done.11, bf16[3,32,32]{2,1,0:T(8,128)(2,1)} %param.6, bf16[32,64,64,64]{3,0,2,1:T(8,128)(2,1)} %fusion.74.clone.5), kind=kOutput, calls=%fused_computation.14 | convolution fusion | flops 1107296256 | bytes 83894400 | tf_op jit(solution)/shard_map/cd,cijk->dijk/dot_general | solution.py:38
  (79 shorter events, 406.6 us)
Async XLA Ops:
  0.0 59.5 %copy-start.9 = (f32[3,3,17]{2,1,0:T(4,128)S(1)}, f32[3,3,17]{2,1,0:T(4,128)}, u32[]{:S(2)}) copy-start(f32[3,3,17]{2,1,0:T(4,128)} %param.5) | copy-start | bytes 1840
  7.4 53.4 %collective-permute-start = (bf16[32,8,64,64]{3,2,1,0:T(8,128)(2,1)}, bf16[32,8,64,64]{3,2,1,0:T(8,128)(2,1)}, u32[]{:S(2)}, u32[]{:S(2)}) collective-permute-start(bf16[32,8,64,64]{3,2,1,0:T(8,128)(2,1)} %get-tuple-element.30), channel_id=1, source_target_pairs={{0,1},{2,3},{4,5},{6,7},{8,9},{10,11},{12,13},{14,15},{16,17},{18,... | collective-permute-start | bytes 6291464 | tf_op jit(solution)/shard_map/ppermute | solution.py:22
  11.2 74.8 %collective-permute-start.1 = (bf16[32,8,64,64]{3,2,1,0:T(8,128)(2,1)}, bf16[32,8,64,64]{3,2,1,0:T(8,128)(2,1)}, u32[]{:S(2)}, u32[]{:S(2)}) collective-permute-start(bf16[32,8,64,64]{3,2,1,0:T(8,128)(2,1)} %get-tuple-element.31), channel_id=1, source_target_pairs={{1,0},{3,2},{5,4},{7,6},{9,8},{11,10},{13,12},{15,14},{17,16},{19,... | collective-permute-start | bytes 6291464 | tf_op jit(solution)/shard_map/ppermute | solution.py:23
  166.7 93.3 %collective-permute-start.2 = (bf16[32,64,8,64]{3,1,2,0:T(8,128)(2,1)S(1)}, bf16[32,64,8,64]{3,1,2,0:T(8,128)(2,1)}, u32[]{:S(2)}, u32[]{:S(2)}) collective-permute-start(bf16[32,64,8,64]{3,1,2,0:T(8,128)(2,1)S(1)} %get-tuple-element.28), channel_id=1, source_target_pairs={{0,2},{2,4},{4,6},{1,3},{3,5},{5,7},{8,10},{10,12},{12,14},{9,11},... | collective-permute-start | bytes 6291464 | tf_op jit(solution)/shard_map/ppermute | solution.py:22
  170.2 93.5 %collective-permute-start.3 = (bf16[32,64,8,64]{3,1,2,0:T(8,128)(2,1)S(1)}, bf16[32,64,8,64]{3,1,2,0:T(8,128)(2,1)}, u32[]{:S(2)}, u32[]{:S(2)}) collective-permute-start(bf16[32,64,8,64]{3,1,2,0:T(8,128)(2,1)S(1)} %get-tuple-element.29), channel_id=1, source_target_pairs={{2,0},{4,2},{6,4},{3,1},{5,3},{7,5},{10,8},{12,10},{14,12},{11,9},... | collective-permute-start | bytes 6291464 | tf_op jit(solution)/shard_map/ppermute | solution.py:23
  328.7 94.2 %collective-permute-start.4 = (bf16[32,64,64,8]{2,3,1,0:T(8,128)(2,1)S(1)}, bf16[32,64,64,8]{2,3,1,0:T(8,128)(2,1)}, u32[]{:S(2)}, u32[]{:S(2)}) collective-permute-start(bf16[32,64,64,8]{2,3,1,0:T(8,128)(2,1)S(1)} %get-tuple-element.26), channel_id=1, source_target_pairs={{0,8},{8,16},{16,24},{1,9},{9,17},{17,25},{2,10},{10,18},{18,26},{... | collective-permute-start | bytes 6291464 | tf_op jit(solution)/shard_map/ppermute | solution.py:22
  334.7 94.8 %collective-permute-start.5 = (bf16[32,64,64,8]{2,3,1,0:T(8,128)(2,1)S(1)}, bf16[32,64,64,8]{2,3,1,0:T(8,128)(2,1)}, u32[]{:S(2)}, u32[]{:S(2)}) collective-permute-start(bf16[32,64,64,8]{2,3,1,0:T(8,128)(2,1)S(1)} %get-tuple-element.27), channel_id=1, source_target_pairs={{8,0},{16,8},{24,16},{9,1},{17,9},{25,17},{10,2},{18,10},{26,18},{... | collective-permute-start | bytes 6291464 | tf_op jit(solution)/shard_map/ppermute | solution.py:23
  458.0 47.9 %copy-start.8 = (bf16[80,64]{0,1:T(8,128)(2,1)S(1)}, bf16[80,64]{0,1:T(8,128)(2,1)}, u32[]{:S(2)}) copy-start(bf16[80,64]{0,1:T(8,128)(2,1)} %get-tuple-element.11) | copy-start | bytes 30724
  717.5 9.0 collective-permute-start.6
  721.8 9.2 collective-permute-start.7
  821.4 94.6 %collective-permute-start.8 = (bf16[32,64,8,64]{3,1,2,0:T(8,128)(2,1)S(1)}, bf16[32,64,8,64]{3,1,2,0:T(8,128)(2,1)}, u32[]{:S(2)}, u32[]{:S(2)}) collective-permute-start(bf16[32,64,8,64]{3,1,2,0:T(8,128)(2,1)S(1)} %get-tuple-element.22), channel_id=1, source_target_pairs={{0,2},{2,4},{4,6},{1,3},{3,5},{5,7},{8,10},{10,12},{12,14},{9,11},... | collective-permute-start | bytes 6291464 | tf_op jit(solution)/shard_map/ppermute | solution.py:22
  824.7 123.3 %copy-start.6 = (bf16[80,64]{0,1:T(8,128)(2,1)S(1)}, bf16[80,64]{0,1:T(8,128)(2,1)}, u32[]{:S(2)}) copy-start(bf16[80,64]{0,1:T(8,128)(2,1)} %get-tuple-element.10) | copy-start | bytes 30724
  824.7 94.6 %collective-permute-start.9 = (bf16[32,64,8,64]{3,1,2,0:T(8,128)(2,1)S(1)}, bf16[32,64,8,64]{3,1,2,0:T(8,128)(2,1)}, u32[]{:S(2)}, u32[]{:S(2)}) collective-permute-start(bf16[32,64,8,64]{3,1,2,0:T(8,128)(2,1)S(1)} %get-tuple-element.23), channel_id=1, source_target_pairs={{2,0},{4,2},{6,4},{3,1},{5,3},{7,5},{10,8},{12,10},{14,12},{11,9},... | collective-permute-start | bytes 6291464 | tf_op jit(solution)/shard_map/ppermute | solution.py:23
  984.3 91.1 %collective-permute-start.10 = (bf16[32,64,64,8]{2,3,1,0:T(8,128)(2,1)S(1)}, bf16[32,64,64,8]{2,3,1,0:T(8,128)(2,1)}, u32[]{:S(2)}, u32[]{:S(2)}) collective-permute-start(bf16[32,64,64,8]{2,3,1,0:T(8,128)(2,1)S(1)} %get-tuple-element.20), channel_id=1, source_target_pairs={{0,8},{8,16},{16,24},{1,9},{9,17},{17,25},{2,10},{10,18},{18,26},{... | collective-permute-start | bytes 6291464 | tf_op jit(solution)/shard_map/ppermute | solution.py:22
  988.4 93.2 %collective-permute-start.11 = (bf16[32,64,64,8]{2,3,1,0:T(8,128)(2,1)S(1)}, bf16[32,64,64,8]{2,3,1,0:T(8,128)(2,1)}, u32[]{:S(2)}, u32[]{:S(2)}) collective-permute-start(bf16[32,64,64,8]{2,3,1,0:T(8,128)(2,1)S(1)} %get-tuple-element.21), channel_id=1, source_target_pairs={{8,0},{16,8},{24,16},{9,1},{17,9},{25,17},{10,2},{18,10},{26,18},{... | collective-permute-start | bytes 6291464 | tf_op jit(solution)/shard_map/ppermute | solution.py:23
  1110.0 48.0 %copy-start.5 = (bf16[80,64]{0,1:T(8,128)(2,1)S(1)}, bf16[80,64]{0,1:T(8,128)(2,1)}, u32[]{:S(2)}) copy-start(bf16[80,64]{0,1:T(8,128)(2,1)} %get-tuple-element.8) | copy-start | bytes 30724
  1364.0 8.1 collective-permute-start.12
  1367.2 9.2 collective-permute-start.13
  1466.9 94.8 %collective-permute-start.14 = (bf16[32,64,8,64]{3,1,2,0:T(8,128)(2,1)S(1)}, bf16[32,64,8,64]{3,1,2,0:T(8,128)(2,1)}, u32[]{:S(2)}, u32[]{:S(2)}) collective-permute-start(bf16[32,64,8,64]{3,1,2,0:T(8,128)(2,1)S(1)} %get-tuple-element.16), channel_id=1, source_target_pairs={{0,2},{2,4},{4,6},{1,3},{3,5},{5,7},{8,10},{10,12},{12,14},{9,11},... | collective-permute-start | bytes 6291464 | tf_op jit(solution)/shard_map/ppermute | solution.py:22
  1469.2 124.5 %copy-start.3 = (bf16[80,64]{0,1:T(8,128)(2,1)S(1)}, bf16[80,64]{0,1:T(8,128)(2,1)}, u32[]{:S(2)}) copy-start(bf16[80,64]{0,1:T(8,128)(2,1)} %get-tuple-element.7) | copy-start | bytes 30724
  1469.2 95.8 %collective-permute-start.15 = (bf16[32,64,8,64]{3,1,2,0:T(8,128)(2,1)S(1)}, bf16[32,64,8,64]{3,1,2,0:T(8,128)(2,1)}, u32[]{:S(2)}, u32[]{:S(2)}) collective-permute-start(bf16[32,64,8,64]{3,1,2,0:T(8,128)(2,1)S(1)} %get-tuple-element.17), channel_id=1, source_target_pairs={{2,0},{4,2},{6,4},{3,1},{5,3},{7,5},{10,8},{12,10},{14,12},{11,9},... | collective-permute-start | bytes 6291464 | tf_op jit(solution)/shard_map/ppermute | solution.py:23
  1629.9 91.0 %collective-permute-start.16 = (bf16[32,64,64,8]{2,3,1,0:T(8,128)(2,1)S(1)}, bf16[32,64,64,8]{2,3,1,0:T(8,128)(2,1)}, u32[]{:S(2)}, u32[]{:S(2)}) collective-permute-start(bf16[32,64,64,8]{2,3,1,0:T(8,128)(2,1)S(1)} %get-tuple-element.14), channel_id=1, source_target_pairs={{0,8},{8,16},{16,24},{1,9},{9,17},{17,25},{2,10},{10,18},{18,26},{... | collective-permute-start | bytes 6291464 | tf_op jit(solution)/shard_map/ppermute | solution.py:22
  1633.7 93.4 %collective-permute-start.17 = (bf16[32,64,64,8]{2,3,1,0:T(8,128)(2,1)S(1)}, bf16[32,64,64,8]{2,3,1,0:T(8,128)(2,1)}, u32[]{:S(2)}, u32[]{:S(2)}) collective-permute-start(bf16[32,64,64,8]{2,3,1,0:T(8,128)(2,1)S(1)} %get-tuple-element.15), channel_id=1, source_target_pairs={{8,0},{16,8},{24,16},{9,1},{17,9},{25,17},{10,2},{18,10},{26,18},{... | collective-permute-start | bytes 6291464 | tf_op jit(solution)/shard_map/ppermute | solution.py:23
  1755.6 48.0 %copy-start.2 = (bf16[80,64]{0,1:T(8,128)(2,1)S(1)}, bf16[80,64]{0,1:T(8,128)(2,1)}, u32[]{:S(2)}) copy-start(bf16[80,64]{0,1:T(8,128)(2,1)} %get-tuple-element.5) | copy-start | bytes 30724
  (7 other events, 195.6 us)
where the time goes:
time: 2030 us; the launch traced here: 2020 us
  matrix products  839 us (41%)
  waiting for transfers between devices  560 us (28%)
  local copies, waits for them, and re-layouts  329 us (16%)
  other arithmetic  231 us (11%)
  starting transfers between devices  58.8 us (3%)
    ppermute x9, waiting for transfers between devices, with_halo(): lax.ppermute(upper_planes, axis_name, [(i, i + 1) for i in range(axis_cou...  522 us
    dot_general x3, matrix products, local_layers(): jnp.einsum('cd,cijk->dijk', mix_w[layer_idx], staged, preferred_element_t...  500 us
    dot_general x9, matrix products, local_layers(): jnp.einsum(PASS_FORMS[dim_pos], padded, band_mat, preferred_element_type=...  340 us
    concatenate x8, other arithmetic, with_halo(): return jnp.concatenate([from_below, local_vol, from_above], axis=dim_pos)  229 us
    concatenate x3, local copies, waits for them, and re-layouts, with_halo(): return jnp.concatenate([from_below, local_vol, from_above], axis=dim_pos)  144 us
    unnamed x27, local copies, waits for them, and re-layouts  70.4 us
    slice x9, local copies, waits for them, and re-layouts, with_halo(): lax.slice_in_dim(local_vol, dim_len - halo_width, dim_len, axis=dim_pos)  41 us
  transfers between devices with their start and end apart: 18, of which 16 were waited for; matrix products, arithmetic and copies ran while one was open for 4% of the time, Pallas kernels for 0%

commit v1 on v0

v1 whole, which is shorter than its diff:
```python
import jax
import jax.numpy as jnp
from jax import lax
from jax.experimental import pallas as pl
from jax.experimental.pallas import tpu as pltpu
from jax.sharding import PartitionSpec as P

BF = jnp.bfloat16
F32 = jnp.float32
SLAB = 16
JH = 2
SQRT_HALF = 0.7071067811865476


def lane_iota(shape):
    return lax.broadcasted_iota(jnp.int32, shape, len(shape) - 1)


def pick_taps(index, valid, taps):
    index = jnp.where(valid, index, -1)
    out = jnp.zeros((taps.shape[0],) + index.shape, F32)
    for t in range(taps.shape[1]):
        out = jnp.where(index[None] == t, taps[:, t][:, None, None], out)
    return out.astype(BF)


def grid2(rows, cols):
    return (lax.broadcasted_iota(jnp.int32, (rows, cols), 0), lax.broadcasted_iota(jnp.int32, (rows, cols), 1))


def x_table(taps, last):
    r, q = grid2(128, 256)
    i_out, i_in = r // 8, q // 8
    if last:
        i_in = jnp.where(i_in >= 24, 55 - i_in, i_in)
    t = i_in - i_out
    return pick_taps(t, (t >= 0) & (t <= 16) & (r % 8 == q % 8), taps)


def y_table(taps):
    r, q = grid2(128, 256)
    t = (q // 64) * 8 + q % 8 - (r // 64) * 8 - r % 8
    return pick_taps(t, (t >= 0) & (t <= 16) & ((r // 8) % 8 == (q // 8) % 8), taps)


def z_tables(taps):
    m, n = grid2(256, 256)
    t = m % 64 - n % 64 + 8
    tables = [pick_taps(t, (t >= 0) & (t <= 16) & (m // 64 == n // 64), taps)]
    for v in range(4):
        k = jnp.where(m < 128, -8, 64) + m % 8
        t = k - n % 64 + 8
        ok = ((m // 64) % 2 == (n // 64) % 2) & ((m // 8) % 8 == 2 * v + n // 128)
        tables.append(pick_taps(t, (t >= 0) & (t <= 16) & ok, taps))
    return jnp.stack(tables, axis=1)


def mix_table(mix_w):
    r, q = grid2(256, 32)
    spread = (r // 8 == q).astype(BF)
    full = jnp.einsum("rd,lcd,qc->lrq", spread, mix_w, spread, preferred_element_type=F32)
    r, q = grid2(256, 256)
    return jnp.where((r % 8 == q % 8)[None], full, 0.0).astype(BF)


def cost(flops):
    return pl.CostEstimate(flops=flops, bytes_accessed=8 << 20, transcendentals=0)


def params():
    return pltpu.CompilerParams(vmem_limit_bytes=60 << 20)


def relayout_in(volume, xi):
    C, I, J, K = volume.shape
    n_slab, cb = I // SLAB, 8

    def body(xi_ref, x_ref, o_ref):
        flip = xi_ref[0]
        for tp in range(SLAB // 2):
            rows = []
            for t in (2 * tp, 2 * tp + 1):
                a = x_ref[:, jnp.where(flip == 1, SLAB - 1 - t, t)].astype(F32)
                a = jnp.concatenate([a[:, : J // 2], a[:, J // 2 :]], axis=2)
                rows.append(a.reshape(cb, 4, 8, 128))
            o_ref[:, :, 16 * tp : 16 * tp + 16, :] = jnp.concatenate(rows, axis=2).astype(BF)

    return pl.pallas_call(
        body,
        grid_spec=pltpu.PrefetchScalarGridSpec(
            num_scalar_prefetch=1,
            grid=(n_slab, C // cb),
            in_specs=[pl.BlockSpec((cb, SLAB, J, K), lambda s, g, f: (g, jnp.where(f[0] == 1, n_slab - 1 - s, s), 0, 0))],
            out_specs=pl.BlockSpec((cb, 4, SLAB * 8, 128), lambda s, g, f: (g, 0, s, 0)),
        ),
        out_shape=jax.ShapeDtypeStruct((C, 4, I * 8, 128), BF),
        compiler_params=params(),
        cost_estimate=cost(1 << 24),
        name="relayout_in",
    )(xi, volume)


def relayout_out(vol, xi, shape):
    C, I, J, K = shape
    cb = 2

    def body(xi_ref, v_ref, o_ref):
        flip = xi_ref[0]
        for tp in range(I // 2):
            a = v_ref[:, :, 16 * tp : 16 * tp + 16, :].astype(F32)
            for u in range(2):
                t = 2 * tp + u
                b = a[:, :, 8 * u : 8 * u + 8, :].reshape(cb, 32, 128)
                b = jnp.concatenate([b[:, :, :64], b[:, :, 64:]], axis=1).astype(BF)
                o_ref[:, jnp.where(flip == 1, I - 1 - t, t)] = b

    return pl.pallas_call(
        body,
        grid_spec=pltpu.PrefetchScalarGridSpec(
            num_scalar_prefetch=1,
            grid=(C // cb,),
            in_specs=[pl.BlockSpec((cb, 4, I * 8, 128), lambda g, f: (g, 0, 0, 0))],
            out_specs=pl.BlockSpec((cb, I, J, K), lambda g, f: (g, 0, 0, 0)),
        ),
        out_shape=jax.ShapeDtypeStruct(shape, BF),
        compiler_params=params(),
        cost_estimate=cost(1 << 26),
        name="relayout_out",
    )(xi, vol)


def x_slab(a, vol, row0, u1, up, dn, C):
    per = 2

    def step(it, _):
        low = lane_iota((128, 128)) < 64
        for q in range(per):
            pair = it * per + q
            ends = []
            for c in (2 * pair, 2 * pair + 1):
                got = []
                for jp in range(2):
                    cols = [vol[c, 2 * jp + b, pl.ds(row0, 256), :] for b in range(2)]
                    u = jnp.dot(a, jnp.concatenate(cols, axis=1), preferred_element_type=F32)
                    u1[c, 2 * jp] = u[:, :128].astype(BF)
                    u1[c, 2 * jp + 1] = u[:, 128:].astype(BF)
                    got.append(u[:, :128] if jp == 0 else u[:, 128:])
                ends.append(got)
            up[pair] = jnp.where(low, pltpu.roll(ends[0][1], 64, 1), ends[1][1]).astype(BF)
            dn[pair] = jnp.where(low, ends[0][0], pltpu.roll(ends[1][0], 64, 1)).astype(BF)
        return 0

    lax.fori_loop(0, C // 2 // per, step, 0)


def y_slab(a, u_ref, b_ref, t_ref, o_ref, up_ref, dn_ref, C):
    def step(pair, _):
        low = lane_iota((128, 128)) < 64
        slot = (lane_iota((2, 16, 128)) % 64) // 8
        c0, c1 = 2 * pair, 2 * pair + 1
        b, t = b_ref[pair].astype(F32), t_ref[pair].astype(F32)
        first = [u_ref[c, 0].astype(F32) for c in (c0, c1)]
        final = [u_ref[c, 3].astype(F32) for c in (c0, c1)]
        lead = [
            jnp.where(low, b, pltpu.roll(final[0], 64, 1)).astype(BF),
            pltpu.roll(jnp.where(low, final[1], b), 64, 1).astype(BF),
        ]
        tail = [
            pltpu.roll(jnp.where(low, t, first[0]), 64, 1).astype(BF),
            jnp.where(low, pltpu.roll(first[1], 64, 1), t).astype(BF),
        ]
        out_rows = pl.ds(pl.multiple_of(16 * pair, 16), 16)
        for g in range(2):
            rows = slice(64 * g, 64 * g + 64)
            for w in range(2):
                cols = []
                for n, c in enumerate((c0, c1)):
                    own = [u_ref[c, jb, rows, :] for jb in range(1, 3)]
                    if w == 0:
                        blocks = [lead[n][rows], u_ref[c, 0, rows, :]] + own
                    else:
                        blocks = own + [u_ref[c, 3, rows, :], tail[n][rows]]
                    cols.append(jnp.concatenate(blocks, axis=0))
                out = jnp.dot(a, jnp.concatenate(cols, axis=1), preferred_element_type=F32)
                out = out.reshape(2, 8, 8, 256)
                out = jnp.concatenate([out[..., :128], out[..., 128:]], axis=2)
                o_ref[2 * w : 2 * w + 2, 8 * g : 8 * g + 8, out_rows, :] = out.astype(BF)
                up = dn = None
                for i in range(8):
                    piece = out[:, i].reshape(32, 128)
                    ru = pltpu.roll(piece, (8 * i + 72) % 128, 1).reshape(2, 16, 128)
                    rd = (piece if i == 0 else pltpu.roll(piece, 8 * i, 1)).reshape(2, 16, 128)
                    up = ru if up is None else jnp.where(slot == i, ru, up)
                    dn = rd if dn is None else jnp.where(slot == i, rd, dn)
                up_ref[2 * w : 2 * w + 2, g, out_rows, :] = up.astype(BF)
                dn_ref[2 * w : 2 * w + 2, g, out_rows, :] = dn.astype(BF)
        return 0

    lax.fori_loop(0, C // 2, step, 0)


def z_slab(z_ref, w_ref, bias_ref, u_ref, b_ref, t_ref, vol, row0, C):
    def step(g, _):
        jb, hi = g // 2, g % 2
        w = w_ref[...]
        bias = bias_ref[...].reshape(C, 8, 128)
        bias = jnp.concatenate([bias, bias], axis=1)
        halo = jnp.concatenate([b_ref[jb, hi], t_ref[jb, hi]], axis=1)
        for p in range(4):
            lhs = jnp.concatenate([u_ref[jb, 8 * hi + 2 * p], u_ref[jb, 8 * hi + 2 * p + 1]], axis=1)
            u3 = jnp.dot(lhs, z_ref[0], preferred_element_type=F32)
            u3 = u3 + jnp.dot(halo, z_ref[1 + p], preferred_element_type=F32)
            m = jnp.dot(w, u3.astype(BF), preferred_element_type=F32).reshape(C, 8, 256)
            m = jnp.concatenate([m[..., :128], m[..., 128:]], axis=1) + bias
            gelu = 0.5 * m * (1.0 + lax.erf(m * SQRT_HALF))
            rows = pl.ds(pl.multiple_of(row0 + 64 * hi + 16 * p, 16), 16)
            v = vol[:, jb, rows, :].astype(F32)
            vol[:, jb, rows, :] = (v + gelu).astype(BF)
        return 0

    lax.fori_loop(0, 8, step, 0)


def fused_layers(v_in, xt, yt, zt, mt, bt, ny, nz):
    C, rows = v_in.shape[0], v_in.shape[2]
    L = xt.shape[0]
    S = rows // 128
    N = L * S
    R = 4
    edge = 64 + rows

    def body(vin, ax, ay, az, am, ab, vout, vol, far, u1, u2, ysend, yrecv, zsend, zrecv,
             in_sem, out_sem, far_ss, far_rs, ys_sem, yr_sem, zs_sem, zr_sem):
        xi, yi, zi = (lax.axis_index(a) for a in ("x", "y", "z"))

        def remote(src, dst, ss, rs, axis, idx):
            return pltpu.make_async_remote_copy(
                src_ref=src, dst_ref=dst, send_sem=ss, recv_sem=rs, device_id={axis: idx}, device_id_type=pl.DeviceIdType.MESH
            )

        def ports(axis, pos, count):
            return ((pos < count - 1, pos + 1, pos > 0), (pos > 0, pos - 1, pos < count - 1))

        def link(axis, pos, count, send, recv, ss, rs):
            info = ports(axis, pos, count)

            def copy(d, n):
                a, b = n % 2, n % R
                return remote(send.at[d, a], recv.at[d, b], ss.at[d, a], rs.at[d, b], axis, info[d][1])

            def start(n):
                for d in range(2):
                    @pl.when(info[d][0])
                    def _():
                        copy(d, n).start()

            def wait_send(n):
                for d in range(2):
                    @pl.when(info[d][0])
                    def _():
                        copy(d, n).wait_send()

            def wait_recv(n):
                for d in range(2):
                    @pl.when(info[d][2])
                    def _():
                        copy(d, n).wait_recv()

            return start, wait_send, wait_recv

        y_start, y_wait_send, y_wait_recv = link("y", yi, ny, ysend, yrecv, ys_sem, yr_sem)
        z_start, z_wait_send, z_wait_recv = link("z", zi, nz, zsend, zrecv, zs_sem, zr_sem)

        def far_copy(l):
            a = l % 2
            return remote(vol.at[:, :, pl.ds(edge - 64, 64), :], far.at[a], far_ss.at[a], far_rs.at[a], "x", 1 - xi)

        def in_copy(s):
            return pltpu.make_async_copy(vin.at[:, :, pl.ds(128 * s, 128), :], vol.at[:, :, pl.ds(64 + 128 * s, 128), :], in_sem.at[s])

        def out_copy(s):
            at = pl.multiple_of(128 * s, 128)
            return pltpu.make_async_copy(vol.at[:, :, pl.ds(64 + at, 128), :], vout.at[:, :, pl.ds(at, 128), :], out_sem.at[s])

        for s in range(S):
            in_copy(s).start()
        barrier = pltpu.get_barrier_semaphore()
        pl.semaphore_signal(barrier, inc=1, device_id={"x": 1 - xi}, device_id_type=pl.DeviceIdType.MESH)
        for axis, pos, count in (("y", yi, ny), ("z", zi, nz)):
            for ok, idx, _ in ports(axis, pos, count):
                @pl.when(ok)
                def _():
                    pl.semaphore_signal(barrier, inc=1, device_id={axis: idx}, device_id_type=pl.DeviceIdType.MESH)
        greet = 1
        for pos, count in ((yi, ny), (zi, nz)):
            greet = greet + (pos > 0).astype(jnp.int32) + (pos < count - 1).astype(jnp.int32)
        pl.semaphore_wait(barrier, greet)

        def zero_margin(c, _):
            for jb in range(4):
                vol[c, jb, 0:64, :] = jnp.zeros((64, 128), BF)
            return 0

        lax.fori_loop(0, C, zero_margin, 0)
        for recv, pos, count in ((yrecv, yi, ny), (zrecv, zi, nz)):
            for d, alone in ((0, pos == 0), (1, pos == count - 1)):
                @pl.when(alone)
                def _():
                    def zero(r, _):
                        for j in range(recv.shape[2]):
                            recv[d, r, j] = jnp.zeros(recv.shape[3:], BF)
                        return 0

                    lax.fori_loop(0, R, zero, 0)

        def stage(n, _):
            @pl.when(n < N)
            def _():
                l, s = n // S, n % S

                @pl.when(n == 0)
                def _():
                    in_copy(0).wait()
                    in_copy(1).wait()

                @pl.when(n == 1)
                def _():
                    for q in range(2, S):
                        in_copy(q).wait()
                    far_copy(0).start()

                @pl.when(s == S - 1)
                def _():
                    far_copy(l).wait()

                    def bring(c, _):
                        for jb in range(4):
                            vol[c, jb, edge : edge + 64, :] = far[l % 2, c, jb]
                        return 0

                    lax.fori_loop(0, C, bring, 0)

                @pl.when(n >= 2)
                def _():
                    y_wait_send(n - 2)

                a = ax[l, (s == S - 1).astype(jnp.int32)]
                x_slab(a, vol, pl.multiple_of(128 * s, 128), u1.at[n % 2], ysend.at[0, n % 2], ysend.at[1, n % 2], C)
                y_start(n)

            @pl.when((n >= 1) & (n <= N))
            def _():
                m = n - 1
                y_wait_recv(m)

                @pl.when(m >= 2)
                def _():
                    z_wait_send(m - 2)

                y_slab(ay[m // S], u1.at[m % 2], yrecv.at[0, m % R], yrecv.at[1, m % R], u2.at[m % 2],
                       zsend.at[0, m % 2], zsend.at[1, m % 2], C)
                z_start(m)

            @pl.when(n >= 2)
            def _():
                m = n - 2
                l, s = m // S, m % S
                z_wait_recv(m)
                z_slab(az.at[l], am.at[l], ab.at[l], u2.at[m % 2], zrecv.at[0, m % R], zrecv.at[1, m % R], vol,
                       64 + 128 * s, C)

                @pl.when((s == S - 1) & (l < L - 1))
                def _():
                    far_copy(l + 1).start()

                @pl.when(l == L - 1)
                def _():
                    out_copy(s).start()

            return 0

        lax.fori_loop(0, N + 2, stage, 0)
        for n in (N - 2, N - 1):
            y_wait_send(n)
            z_wait_send(n)
        for s in range(S):
            out_copy(s).wait()

    vmem = pl.BlockSpec(memory_space=pltpu.VMEM)
    hbm = pl.BlockSpec(memory_space=pltpu.HBM)
    dma = pltpu.SemaphoreType.DMA
    return pl.pallas_call(
        body,
        in_specs=[hbm] + [vmem] * 5,
        out_specs=hbm,
        out_shape=jax.ShapeDtypeStruct(v_in.shape, BF),
        scratch_shapes=[
            pltpu.VMEM((C, 4, rows + 128, 128), BF),
            pltpu.VMEM((2, C, 4, 64, 128), BF),
            pltpu.VMEM((2, C, 4, 128, 128), BF),
            pltpu.VMEM((2, 4, SLAB, 8 * C, 128), BF),
            pltpu.VMEM((2, 2, C // 2, 128, 128), BF),
            pltpu.VMEM((2, R, C // 2, 128, 128), BF),
            pltpu.VMEM((2, 2, 4, 2, 8 * C, 128), BF),
            pltpu.VMEM((2, R, 4, 2, 8 * C, 128), BF),
            dma((S,)),
            dma((S,)),
            dma((2,)),
            dma((2,)),
            dma((2, 2)),
            dma((2, R)),
            dma((2, 2)),
            dma((2, R)),
        ],
        compiler_params=pltpu.CompilerParams(vmem_limit_bytes=67043328, collective_id=0, has_side_effects=True),
        cost_estimate=cost(1 << 32),
        name="fused_layers",
    )(v_in, xt, yt, zt, mt, bt)


def solution(mesh):
    ny, nz = mesh.shape["y"], mesh.shape["z"]

    def local_layers(volume, filter_taps, mix_w, mix_bias):
        xi = lax.axis_index("x").astype(jnp.int32)
        xi_arr = xi.reshape(1)
        layers = filter_taps.shape[0]
        taps = filter_taps.astype(BF).astype(F32)
        taps_x = jnp.where(xi == 1, taps[:, 0, ::-1], taps[:, 0])
        xt = jnp.stack([x_table(taps_x, False), x_table(taps_x, True)], axis=1)
        yt, zt, mt = y_table(taps[:, 1]), z_tables(taps[:, 2]), mix_table(mix_w)
        bt = jnp.broadcast_to(jnp.repeat(mix_bias, 8, axis=1)[:, :, None], (layers, 256, 128))
        out = fused_layers(relayout_in(volume, xi_arr), xt, yt, zt, mt, bt, ny, nz)
        return relayout_out(out, xi_arr, volume.shape)

    vol_spec = P("batch", "x", "y", "z")
    return jax.shard_map(
        local_layers, mesh=mesh, in_specs=(vol_spec, P(), P(), P()), out_specs=vol_spec, check_vma=False
    )
```

time: 2030 us -> 362 us (0.18)
  matrix products: 839 us -> 2.1 us
  waiting for transfers between devices: 560 us -> 0 us
  Pallas kernels: 0 us -> 329 us
  local copies, waits for them, and re-layouts: 329 us -> 4 us
  other arithmetic: 231 us -> 25.4 us
  starting transfers between devices: 58.8 us -> 0 us
    dot_general x12 -> x1, matrix products: 839 us -> 2.1 us  [mix_table(): jnp.einsum('rd,lcd,qc->lrq', spread, mix_w, spread, preferred_element_typ...]
    ppermute x18 -> x0, waiting for transfers between devices: 560 us -> none  [the longest x9 522 us: with_halo(): lax.ppermute(upper_planes, axis_name, [(i, i + 1) for i in range(axis_cou...]
    pallas_call x0 -> x3, Pallas kernels: none -> 329 us  [the longest x1 285 us: fused_layers(): pl.pallas_call(body, in_specs=[hbm] + [vmem] * 5, out_specs=hbm, out_shap...]
    concatenate x8 -> x0, other arithmetic: 229 us -> none  [with_halo(): return jnp.concatenate([from_below, local_vol, from_above], axis=dim_pos)]
    concatenate x3 -> x0, local copies, waits for them, and re-layouts: 144 us -> none  [with_halo(): return jnp.concatenate([from_below, local_vol, from_above], axis=dim_pos)]
    unnamed x27 -> x54, local copies, waits for them, and re-layouts: 70.4 us -> 0.12 us
    ppermute x18 -> x0, starting transfers between devices: 58.8 us -> none  [the longest x9 34.4 us: with_halo(): lax.ppermute(upper_planes, axis_name, [(i, i + 1) for i in range(axis_cou...]
    ppermute x2 -> x0, local copies, waits for them, and re-layouts: 50.2 us -> none  [the longest x1 25.2 us: with_halo(): lax.ppermute(upper_planes, axis_name, [(i, i + 1) for i in range(axis_cou...]
  transfers between devices with their start and end apart: 18 -> 0, of which waited for: 16 -> 0; matrix products, arithmetic and copies ran while one was open for 4% -> 0% of each run, Pallas kernels for 0% -> 0%
where the time goes in v1:
time: 362 us; the launch traced here: 361 us
  Pallas kernels  329 us (91%)
  other arithmetic  25.4 us (7%)
  local copies, waits for them, and re-layouts  4 us (1%)
    pallas_call x1, Pallas kernels, fused_layers(): pl.pallas_call(body, in_specs=[hbm] + [vmem] * 5, out_specs=hbm, out_shap...  285 us
    pallas_call x1, Pallas kernels, relayout_in(): pl.pallas_call(body, grid_spec=pltpu.PrefetchScalarGridSpec(num_scalar_pr...  23.2 us
    pallas_call x1, Pallas kernels, relayout_out(): pl.pallas_call(body, grid_spec=pltpu.PrefetchScalarGridSpec(num_scalar_pr...  21.1 us
    unnamed x4, other arithmetic  10.1 us
    eq x4, other arithmetic, pick_taps(): out = jnp.where(index[None] == t, taps[:, t][:, None, None], out)  9.71 us

profile of v1, /device:TPU:98, one launch (start us, length us, event | category | flops | bytes accessed | tf_op | source)
XLA Modules:
  0.0 361.4 jit_solution(13449999200531751665)
XLA Ops:
  0.2 0.7 convert_convert_fusion
  1.1 0.5 slice_reduce_fusion.50
  1.5 1.0 slice_reduce_fusion.16
  2.6 0.5 slice_reduce_fusion.33
  3.0 0.8 broadcast_in_dim.1729
  3.8 0.1 broadcast_in_dim.1730
  3.9 0.9 broadcast_in_dim.1731.ab
  4.8 1.8 fusion.81
  6.7 1.1 broadcast_compare_fusion.30
  7.8 1.3 select_convert_fusion.5.ay
  9.1 0.5 select_convert_fusion.6
  9.6 0.4 fusion.138
  10.1 0.5 select_convert_fusion.7
  10.6 0.8 pad_maximum_fusion.ax
  11.4 6.3 %fusion.80 = (pred[256,256]{1,0:T(8,128)(4,1)S(1)}, pred[256,256]{1,0:T(8,128)(4,1)S(1)}, pred[256,256]{1,0:T(8,128)(4,1)S(1)}, pred[256,256]{1,0:T(8,128)(4,1)S...) fusion(pred[256,256]{1,0:T(8,128)(4,1)S(1)} %get-tuple-element., ...), kind=kLoop, calls=%fused_computation.126 | loop fusion | flops 6225920 | bytes 5641728 | tf_op jit(solution)/shard_map/eq | solution.py:23
  17.7 2.1 fusion.am
  20.0 3.0 fusion.1
  23.1 2.9 fusion.2
  26.0 2.4 fusion.3
  28.6 1.7 fusion.4
  30.3 1.7 fusion.5.az
  32.0 23.2 %relayout_in.1.vin = bf16[32,4,512,128]{3,2,1,0:T(8,128)(2,1)} custom-call(s32[1]{0:T(128)} %bitcast.xi_ref, bf16[32,64,64,64]{3,2,1,0:T(8,128)(2,1)} %x_ref.1), custom_call_target="tpu_custom_call" | custom-call | flops 16777216 | bytes 8388608 | tf_op jit(solution)/shard_map/relayout_in/pallas_call | solution.py:88
  55.2 285.0 %fused_layers.1.v_ref = bf16[32,4,512,128]{3,2,1,0:T(8,128)(2,1)} custom-call(bf16[32,4,512,128]{3,2,1,0:T(8,128)(2,1)} %relayout_in.1.vin, bf16[3,2,128,256]{3,2,1,0:T(8,128)(2,1)} %pad_maximum_fusion.ax, bf16[3,128,256]{2,1,0:T(8,128)(2,1)} %select_convert_fusion.5.ay, bf16[3,5,256,256]{3,2,1,0:T(8,128)(2,1)} %fusion.5.az, bf16[3,256,256]{2,1,0:T(8,128)(2,1)} %fusion.am, ...), custom_call_target="tpu_custom_call" | custom-call | flops 4294967296 | bytes 8388608 | tf_op jit(solution)/shard_map/fused_layers/pallas_call | solution.py:392
  340.2 21.1 %relayout_out.1 = bf16[32,64,64,64]{3,2,1,0:T(8,128)(2,1)} custom-call(s32[1]{0:T(128)} %bitcast.xi_ref, bf16[32,4,512,128]{3,2,1,0:T(8,128)(2,1)} %fused_layers.1.v_ref), custom_call_target="tpu_custom_call" | custom-call | flops 67108864 | bytes 8388608 | tf_op jit(solution)/shard_map/relayout_out/pallas_call | solution.py:117
  (71 shorter events, 0.3 us)
Async XLA Ops:
  0.0 9.6 %copy-start.25 = (pred[256]{0:T(512)(128)(4,1)}, pred[256]{0:T(512)(128)(4,1)S(1)}, u32[]{:S(2)}) copy-start(pred[256]{0:T(512)(128)(4,1)S(1)} %fusion.168) | copy-start | bytes 772
  0.1 9.5 %copy-start.23 = (pred[256]{0:T(512)(128)(4,1)}, pred[256]{0:T(512)(128)(4,1)S(1)}, u32[]{:S(2)}) copy-start(pred[256]{0:T(512)(128)(4,1)S(1)} %get-tuple-element.282) | copy-start | bytes 772
  0.1 9.5 %copy-start.24 = (pred[256]{0:T(512)(128)(4,1)}, pred[256]{0:T(512)(128)(4,1)S(1)}, u32[]{:S(2)}) copy-start(pred[256]{0:T(512)(128)(4,1)S(1)} %get-tuple-element.295) | copy-start | bytes 772
  0.1 9.5 %copy-start.20 = (s32[256]{0:T(256)}, s32[256]{0:T(256)S(1)}, u32[]{:S(2)}) copy-start(s32[256]{0:T(256)S(1)} %get-tuple-element.291) | copy-start | bytes 3076
  0.2 9.4 %copy-start.22 = (s32[256]{0:T(256)}, s32[256]{0:T(256)S(1)}, u32[]{:S(2)}) copy-start(s32[256]{0:T(256)S(1)} %get-tuple-element.296) | copy-start | bytes 3076
  0.2 9.4 %copy-start.21 = (s32[256]{0:T(256)}, s32[256]{0:T(256)S(1)}, u32[]{:S(2)}) copy-start(s32[256]{0:T(256)S(1)} %get-tuple-element.278) | copy-start | bytes 3076
  17.7 5.3 %copy-start.3 = (bf16[3]{0:T(256)(128)(2,1)S(1)}, bf16[3]{0:T(256)(128)(2,1)}, u32[]{:S(2)}) copy-start(bf16[3]{0:T(256)(128)(2,1)} %get-tuple-element.5) | copy-start | bytes 22
  17.7 5.3 %copy-start.4 = (bf16[3]{0:T(256)(128)(2,1)S(1)}, bf16[3]{0:T(256)(128)(2,1)}, u32[]{:S(2)}) copy-start(bf16[3]{0:T(256)(128)(2,1)} %get-tuple-element.6) | copy-start | bytes 22
  19.8 6.2 %copy-start.2 = (pred[256,256]{1,0:T(8,128)(4,1)S(1)}, pred[256,256]{1,0:T(8,128)(4,1)}, u32[]{:S(2)}) copy-start(pred[256,256]{1,0:T(8,128)(4,1)} %get-tuple-element.166) | copy-start | bytes 196612
  19.8 8.6 %copy-start.1 = (pred[256,256]{1,0:T(8,128)(4,1)S(1)}, pred[256,256]{1,0:T(8,128)(4,1)}, u32[]{:S(2)}) copy-start(pred[256,256]{1,0:T(8,128)(4,1)} %get-tuple-element.164) | copy-start | bytes 196612
  19.8 8.6 %copy-start.7 = (bf16[3]{0:T(256)(128)(2,1)S(1)}, bf16[3]{0:T(256)(128)(2,1)}, u32[]{:S(2)}) copy-start(bf16[3]{0:T(256)(128)(2,1)} %get-tuple-element.9) | copy-start | bytes 22
  19.9 8.6 %copy-start.8 = (bf16[3]{0:T(256)(128)(2,1)S(1)}, bf16[3]{0:T(256)(128)(2,1)}, u32[]{:S(2)}) copy-start(bf16[3]{0:T(256)(128)(2,1)} %get-tuple-element.10) | copy-start | bytes 22
  19.9 8.6 %copy-start.9 = (bf16[3]{0:T(256)(128)(2,1)S(1)}, bf16[3]{0:T(256)(128)(2,1)}, u32[]{:S(2)}) copy-start(bf16[3]{0:T(256)(128)(2,1)} %get-tuple-element.11) | copy-start | bytes 22
  19.9 8.6 %copy-start.10 = (bf16[3]{0:T(256)(128)(2,1)S(1)}, bf16[3]{0:T(256)(128)(2,1)}, u32[]{:S(2)}) copy-start(bf16[3]{0:T(256)(128)(2,1)} %get-tuple-element.12) | copy-start | bytes 22
  19.9 8.6 %copy-start.11 = (bf16[3]{0:T(256)(128)(2,1)S(1)}, bf16[3]{0:T(256)(128)(2,1)}, u32[]{:S(2)}) copy-start(bf16[3]{0:T(256)(128)(2,1)} %get-tuple-element.13) | copy-start | bytes 22
  19.9 8.6 %copy-start.12 = (bf16[3]{0:T(256)(128)(2,1)S(1)}, bf16[3]{0:T(256)(128)(2,1)}, u32[]{:S(2)}) copy-start(bf16[3]{0:T(256)(128)(2,1)} %get-tuple-element.14) | copy-start | bytes 22
  19.9 8.6 %copy-start.13 = (bf16[3]{0:T(256)(128)(2,1)S(1)}, bf16[3]{0:T(256)(128)(2,1)}, u32[]{:S(2)}) copy-start(bf16[3]{0:T(256)(128)(2,1)} %get-tuple-element.15) | copy-start | bytes 22
  19.9 8.6 %copy-start.14 = (bf16[3]{0:T(256)(128)(2,1)S(1)}, bf16[3]{0:T(256)(128)(2,1)}, u32[]{:S(2)}) copy-start(bf16[3]{0:T(256)(128)(2,1)} %get-tuple-element.16) | copy-start | bytes 22
  19.9 8.6 %copy-start.15 = (bf16[3]{0:T(256)(128)(2,1)S(1)}, bf16[3]{0:T(256)(128)(2,1)}, u32[]{:S(2)}) copy-start(bf16[3]{0:T(256)(128)(2,1)} %get-tuple-element.17) | copy-start | bytes 22
  19.9 8.6 %copy-start.16 = (bf16[3]{0:T(256)(128)(2,1)S(1)}, bf16[3]{0:T(256)(128)(2,1)}, u32[]{:S(2)}) copy-start(bf16[3]{0:T(256)(128)(2,1)} %get-tuple-element.18) | copy-start | bytes 22
  19.9 8.6 %copy-start.17 = (bf16[3]{0:T(256)(128)(2,1)S(1)}, bf16[3]{0:T(256)(128)(2,1)}, u32[]{:S(2)}) copy-start(bf16[3]{0:T(256)(128)(2,1)} %get-tuple-element.19) | copy-start | bytes 22
  20.0 8.6 %copy-start.18 = (bf16[3]{0:T(256)(128)(2,1)S(1)}, bf16[3]{0:T(256)(128)(2,1)}, u32[]{:S(2)}) copy-start(bf16[3]{0:T(256)(128)(2,1)} %get-tuple-element.20) | copy-start | bytes 22
  20.0 8.6 %copy-start.19 = (bf16[3]{0:T(256)(128)(2,1)S(1)}, bf16[3]{0:T(256)(128)(2,1)}, u32[]{:S(2)}) copy-start(bf16[3]{0:T(256)(128)(2,1)} %get-tuple-element.21) | copy-start | bytes 22
  23.1 7.2 %copy-start = (pred[256,256]{1,0:T(8,128)(4,1)S(1)}, pred[256,256]{1,0:T(8,128)(4,1)}, u32[]{:S(2)}) copy-start(pred[256,256]{1,0:T(8,128)(4,1)} %get-tuple-element.56) | copy-start | bytes 196612
  (2 other events, 10.6 us)

commit v2 on v1

--- a/solution.py
+++ b/solution.py
@@ -8,8 +8,9 @@
 BF = jnp.bfloat16
 F32 = jnp.float32
 SLAB = 16
+X_UNROLL, Y_UNROLL = 8, 4
 JH = 2
-SQRT_HALF = 0.7071067811865476
+SQRT_TWO = 1.4142135623730951
 
 
 def lane_iota(shape):
@@ -60,7 +61,7 @@
     spread = (r // 8 == q).astype(BF)
     full = jnp.einsum("rd,lcd,qc->lrq", spread, mix_w, spread, preferred_element_type=F32)
     r, q = grid2(256, 256)
-    return jnp.where((r % 8 == q % 8)[None], full, 0.0).astype(BF)
+    return jnp.where((r % 8 == q % 8)[None], 0.5 * full, 0.0).astype(BF)
 
 
 def cost(flops):
@@ -83,7 +84,9 @@
                 a = x_ref[:, jnp.where(flip == 1, SLAB - 1 - t, t)].astype(F32)
                 a = jnp.concatenate([a[:, : J // 2], a[:, J // 2 :]], axis=2)
                 rows.append(a.reshape(cb, 4, 8, 128))
-            o_ref[:, :, 16 * tp : 16 * tp + 16, :] = jnp.concatenate(rows, axis=2).astype(BF)
+            both = jnp.concatenate(rows, axis=2).astype(BF)
+            for jb in range(4):
+                o_ref[jb, :, 16 * tp : 16 * tp + 16, :] = both[:, jb]
 
     return pl.pallas_call(
         body,
@@ -91,9 +94,9 @@
             num_scalar_prefetch=1,
             grid=(n_slab, C // cb),
             in_specs=[pl.BlockSpec((cb, SLAB, J, K), lambda s, g, f: (g, jnp.where(f[0] == 1, n_slab - 1 - s, s), 0, 0))],
-            out_specs=pl.BlockSpec((cb, 4, SLAB * 8, 128), lambda s, g, f: (g, 0, s, 0)),
+            out_specs=pl.BlockSpec((4, cb, SLAB * 8, 128), lambda s, g, f: (0, g, s, 0)),
         ),
-        out_shape=jax.ShapeDtypeStruct((C, 4, I * 8, 128), BF),
+        out_shape=jax.ShapeDtypeStruct((4, C, I * 8, 128), BF),
         compiler_params=params(),
         cost_estimate=cost(1 << 24),
         name="relayout_in",
@@ -107,10 +110,10 @@
     def body(xi_ref, v_ref, o_ref):
         flip = xi_ref[0]
         for tp in range(I // 2):
-            a = v_ref[:, :, 16 * tp : 16 * tp + 16, :].astype(F32)
+            a = [v_ref[jb, :, 16 * tp : 16 * tp + 16, :].astype(F32) for jb in range(4)]
             for u in range(2):
                 t = 2 * tp + u
-                b = a[:, :, 8 * u : 8 * u + 8, :].reshape(cb, 32, 128)
+                b = jnp.concatenate([q[:, 8 * u : 8 * u + 8, :] for q in a], axis=1)
                 b = jnp.concatenate([b[:, :, :64], b[:, :, 64:]], axis=1).astype(BF)
                 o_ref[:, jnp.where(flip == 1, I - 1 - t, t)] = b
 
@@ -119,7 +122,7 @@
         grid_spec=pltpu.PrefetchScalarGridSpec(
             num_scalar_prefetch=1,
             grid=(C // cb,),
-            in_specs=[pl.BlockSpec((cb, 4, I * 8, 128), lambda g, f: (g, 0, 0, 0))],
+            in_specs=[pl.BlockSpec((4, cb, I * 8, 128), lambda g, f: (0, g, 0, 0))],
             out_specs=pl.BlockSpec((cb, I, J, K), lambda g, f: (g, 0, 0, 0)),
         ),
         out_shape=jax.ShapeDtypeStruct(shape, BF),
@@ -130,7 +133,7 @@
 
 
 def x_slab(a, vol, row0, u1, up, dn, C):
-    per = 2
+    per = X_UNROLL
 
     def step(it, _):
         low = lane_iota((128, 128)) < 64
@@ -140,34 +143,35 @@
             for c in (2 * pair, 2 * pair + 1):
                 got = []
                 for jp in range(2):
-                    cols = [vol[c, 2 * jp + b, pl.ds(row0, 256), :] for b in range(2)]
+                    cols = [vol[2 * jp + b, c, pl.ds(row0, 256), :] for b in range(2)]
                     u = jnp.dot(a, jnp.concatenate(cols, axis=1), preferred_element_type=F32)
-                    u1[c, 2 * jp] = u[:, :128].astype(BF)
-                    u1[c, 2 * jp + 1] = u[:, 128:].astype(BF)
+                    u = u.astype(BF)
+                    u1[c, 2 * jp] = u[:, :128]
+                    u1[c, 2 * jp + 1] = u[:, 128:]
                     got.append(u[:, :128] if jp == 0 else u[:, 128:])
                 ends.append(got)
-            up[pair] = jnp.where(low, pltpu.roll(ends[0][1], 64, 1), ends[1][1]).astype(BF)
-            dn[pair] = jnp.where(low, ends[0][0], pltpu.roll(ends[1][0], 64, 1)).astype(BF)
+            up[pair] = jnp.where(low, pltpu.roll(ends[0][1], 64, 1), ends[1][1])
+            dn[pair] = jnp.where(low, ends[0][0], pltpu.roll(ends[1][0], 64, 1))
         return 0
 
     lax.fori_loop(0, C // 2 // per, step, 0)
 
 
 def y_slab(a, u_ref, b_ref, t_ref, o_ref, up_ref, dn_ref, C):
-    def step(pair, _):
+    def one(pair):
         low = lane_iota((128, 128)) < 64
-        slot = (lane_iota((2, 16, 128)) % 64) // 8
+        slot = (lane_iota((16, 128)) % 64) // 8
         c0, c1 = 2 * pair, 2 * pair + 1
-        b, t = b_ref[pair].astype(F32), t_ref[pair].astype(F32)
-        first = [u_ref[c, 0].astype(F32) for c in (c0, c1)]
-        final = [u_ref[c, 3].astype(F32) for c in (c0, c1)]
+        b, t = b_ref[pair], t_ref[pair]
+        first = [u_ref[c, 0] for c in (c0, c1)]
+        final = [u_ref[c, 3] for c in (c0, c1)]
         lead = [
-            jnp.where(low, b, pltpu.roll(final[0], 64, 1)).astype(BF),
-            pltpu.roll(jnp.where(low, final[1], b), 64, 1).astype(BF),
+            jnp.where(low, b, pltpu.roll(final[0], 64, 1)),
+            pltpu.roll(jnp.where(low, final[1], b), 64, 1),
         ]
         tail = [
-            pltpu.roll(jnp.where(low, t, first[0]), 64, 1).astype(BF),
-            jnp.where(low, pltpu.roll(first[1], 64, 1), t).astype(BF),
+            pltpu.roll(jnp.where(low, t, first[0]), 64, 1),
+            jnp.where(low, pltpu.roll(first[1], 64, 1), t),
         ]
         out_rows = pl.ds(pl.multiple_of(16 * pair, 16), 16)
         for g in range(2):
@@ -183,53 +187,63 @@
                     cols.append(jnp.concatenate(blocks, axis=0))
                 out = jnp.dot(a, jnp.concatenate(cols, axis=1), preferred_element_type=F32)
                 out = out.reshape(2, 8, 8, 256)
-                out = jnp.concatenate([out[..., :128], out[..., 128:]], axis=2)
-                o_ref[2 * w : 2 * w + 2, 8 * g : 8 * g + 8, out_rows, :] = out.astype(BF)
-                up = dn = None
-                for i in range(8):
-                    piece = out[:, i].reshape(32, 128)
-                    ru = pltpu.roll(piece, (8 * i + 72) % 128, 1).reshape(2, 16, 128)
-                    rd = (piece if i == 0 else pltpu.roll(piece, 8 * i, 1)).reshape(2, 16, 128)
-                    up = ru if up is None else jnp.where(slot == i, ru, up)
-                    dn = rd if dn is None else jnp.where(slot == i, rd, dn)
-                up_ref[2 * w : 2 * w + 2, g, out_rows, :] = up.astype(BF)
-                dn_ref[2 * w : 2 * w + 2, g, out_rows, :] = dn.astype(BF)
+                out = jnp.concatenate([out[..., :128], out[..., 128:]], axis=2).astype(BF)
+                o_ref[2 * w : 2 * w + 2, 8 * g : 8 * g + 8, out_rows, :] = out
+                for e in range(2):
+                    up = dn = None
+                    for i in range(8):
+                        ru = pltpu.roll(out[e, i], (8 * i + 72) % 128, 1)
+                        rd = out[e, i] if i == 0 else pltpu.roll(out[e, i], 8 * i, 1)
+                        up = ru if up is None else jnp.where(slot == i, ru, up)
+                        dn = rd if dn is None else jnp.where(slot == i, rd, dn)
+                    up_ref[2 * w + e, g, out_rows, :] = up
+                    dn_ref[2 * w + e, g, out_rows, :] = dn
+
+    def step(it, _):
+        for q in range(Y_UNROLL):
+            one(it * Y_UNROLL + q)
         return 0
 
-    lax.fori_loop(0, C // 2, step, 0)
-
-
-def z_slab(z_ref, w_ref, bias_ref, u_ref, b_ref, t_ref, vol, row0, C):
-    def step(g, _):
-        jb, hi = g // 2, g % 2
-        w = w_ref[...]
-        bias = bias_ref[...].reshape(C, 8, 128)
-        bias = jnp.concatenate([bias, bias], axis=1)
-        halo = jnp.concatenate([b_ref[jb, hi], t_ref[jb, hi]], axis=1)
-        for p in range(4):
-            lhs = jnp.concatenate([u_ref[jb, 8 * hi + 2 * p], u_ref[jb, 8 * hi + 2 * p + 1]], axis=1)
-            u3 = jnp.dot(lhs, z_ref[0], preferred_element_type=F32)
-            u3 = u3 + jnp.dot(halo, z_ref[1 + p], preferred_element_type=F32)
-            m = jnp.dot(w, u3.astype(BF), preferred_element_type=F32).reshape(C, 8, 256)
-            m = jnp.concatenate([m[..., :128], m[..., 128:]], axis=1) + bias
-            gelu = 0.5 * m * (1.0 + lax.erf(m * SQRT_HALF))
-            rows = pl.ds(pl.multiple_of(row0 + 64 * hi + 16 * p, 16), 16)
-            v = vol[:, jb, rows, :].astype(F32)
-            vol[:, jb, rows, :] = (v + gelu).astype(BF)
+    lax.fori_loop(0, C // 2 // Y_UNROLL, step, 0)
+
+
+def z_slab(z_ref, w_ref, bias_ref, u_ref, b_ref, t_ref, vol, row0, u3_ref, C):
+    def z_pair(jb, ip):
+        lhs = jnp.concatenate([u_ref[jb, 2 * ip + q, : 8 * C, :] for q in range(2)], axis=1)
+        halo = jnp.concatenate([b_ref[jb, ip // 4], t_ref[jb, ip // 4]], axis=1)
+        u3 = jnp.dot(lhs, z_ref[0], preferred_element_type=F32)
+        u3 = u3 + jnp.dot(halo, z_ref[1 + ip % 4], preferred_element_type=F32)
+        return u3.astype(BF)
+
+    u3_ref[...] = z_pair(0, 0)
+
+    def step(jb, _):
+        u3 = u3_ref[...]
+        for ip in range(8):
+            ahead = z_pair(jb, ip + 1) if ip < 7 else z_pair(jnp.minimum(jb + 1, 3), 0)
+            bias = bias_ref[...].reshape(C, 8, 128)
+            m = jnp.dot(w_ref[...], u3, preferred_element_type=F32).reshape(C, 8, 256)
+            m = jnp.concatenate([m[..., :128] + bias, m[..., 128:] + bias], axis=1)
+            gelu = m + m * lax.erf(m * SQRT_TWO)
+            rows = pl.ds(pl.multiple_of(row0 + 16 * ip, 16), 16)
+            v = vol[jb, :, rows, :].astype(F32)
+            vol[jb, :, rows, :] = (v + gelu).astype(BF)
+            u3 = ahead
+        u3_ref[...] = u3
         return 0
 
-    lax.fori_loop(0, 8, step, 0)
+    lax.fori_loop(0, 4, step, 0)
 
 
 def fused_layers(v_in, xt, yt, zt, mt, bt, ny, nz):
-    C, rows = v_in.shape[0], v_in.shape[2]
+    C, rows = v_in.shape[1], v_in.shape[2]
     L = xt.shape[0]
     S = rows // 128
     N = L * S
     R = 4
     edge = 64 + rows
 
-    def body(vin, ax, ay, az, am, ab, vout, vol, far, u1, u2, ysend, yrecv, zsend, zrecv,
+    def body(vin, ax, ay, az, am, ab, vout, vol, far, u1, u2, u3, ysend, yrecv, zsend, zrecv,
              in_sem, out_sem, far_ss, far_rs, ys_sem, yr_sem, zs_sem, zr_sem):
         xi, yi, zi = (lax.axis_index(a) for a in ("x", "y", "z"))
 
@@ -298,7 +312,7 @@
 
         def zero_margin(c, _):
             for jb in range(4):
-                vol[c, jb, 0:64, :] = jnp.zeros((64, 128), BF)
+                vol[jb, c, 0:64, :] = jnp.zeros((64, 128), BF)
             return 0
 
         lax.fori_loop(0, C, zero_margin, 0)
@@ -335,7 +349,7 @@
 
                     def bring(c, _):
                         for jb in range(4):
-                            vol[c, jb, edge : edge + 64, :] = far[l % 2, c, jb]
+                            vol[jb, c, edge : edge + 64, :] = far[l % 2, jb, c]
                         return 0
 
                     lax.fori_loop(0, C, bring, 0)
@@ -367,7 +381,7 @@
                 l, s = m // S, m % S
                 z_wait_recv(m)
                 z_slab(az.at[l], am.at[l], ab.at[l], u2.at[m % 2], zrecv.at[0, m % R], zrecv.at[1, m % R], vol,
-                       64 + 128 * s, C)
+                       64 + 128 * s, u3, C)
 
                 @pl.when((s == S - 1) & (l < L - 1))
                 def _():
@@ -395,10 +409,11 @@
         out_specs=hbm,
         out_shape=jax.ShapeDtypeStruct(v_in.shape, BF),
         scratch_shapes=[
-            pltpu.VMEM((C, 4, rows + 128, 128), BF),
-            pltpu.VMEM((2, C, 4, 64, 128), BF),
+            pltpu.VMEM((4, C, rows + 128, 128), BF),
+            pltpu.VMEM((2, 4, C, 64, 128), BF),
             pltpu.VMEM((2, C, 4, 128, 128), BF),
             pltpu.VMEM((2, 4, SLAB, 8 * C, 128), BF),
+            pltpu.VMEM((8 * C, 256), BF),
             pltpu.VMEM((2, 2, C // 2, 128, 128), BF),
             pltpu.VMEM((2, R, C // 2, 128, 128), BF),
             pltpu.VMEM((2, 2, 4, 2, 8 * C, 128), BF),
@@ -429,7 +444,7 @@
         taps_x = jnp.where(xi == 1, taps[:, 0, ::-1], taps[:, 0])
         xt = jnp.stack([x_table(taps_x, False), x_table(taps_x, True)], axis=1)
         yt, zt, mt = y_table(taps[:, 1]), z_tables(taps[:, 2]), mix_table(mix_w)
-        bt = jnp.broadcast_to(jnp.repeat(mix_bias, 8, axis=1)[:, :, None], (layers, 256, 128))
+        bt = jnp.broadcast_to(jnp.repeat(0.5 * mix_bias, 8, axis=1)[:, :, None], (layers, 256, 128))
         out = fused_layers(relayout_in(volume, xi_arr), xt, yt, zt, mt, bt, ny, nz)
         return relayout_out(out, xi_arr, volume.shape)
 

time: 362 us -> 249 us (0.69)
  Pallas kernels: 329 us -> 217 us
    pallas_call x1, Pallas kernels: 285 us -> 172 us  [fused_layers(): pl.pallas_call(body, in_specs=[hbm] + [vmem] * 5, out_specs=hbm, out_shap...]
where the time goes in v2:
time: 249 us; the launch traced here: 248 us
  Pallas kernels  217 us (87%)
  other arithmetic  25.3 us (10%)
  local copies, waits for them, and re-layouts  3.32 us (1%)
    pallas_call x1, Pallas kernels, fused_layers(): pl.pallas_call(body, in_specs=[hbm] + [vmem] * 5, out_specs=hbm, out_shap...  172 us
    pallas_call x1, Pallas kernels, relayout_in(): pl.pallas_call(body, grid_spec=pltpu.PrefetchScalarGridSpec(num_scalar_pr...  23.3 us
    pallas_call x1, Pallas kernels, relayout_out(): pl.pallas_call(body, grid_spec=pltpu.PrefetchScalarGridSpec(num_scalar_pr...  21.1 us
    eq x4, other arithmetic, pick_taps(): out = jnp.where(index[None] == t, taps[:, t][:, None, None], out)  9.71 us
    unnamed x4, other arithmetic  9.34 us

profile of v2, /device:TPU:98, one launch (start us, length us, event | category | flops | bytes accessed | tf_op | source)
XLA Modules:
  0.0 248.1 jit_solution(14923688853429010822)
XLA Ops:
  0.1 0.7 broadcast_multiply_fusion
  0.9 0.7 convert_convert_fusion
  1.7 0.5 slice_reduce_fusion.50
  2.2 1.0 slice_reduce_fusion.16
  3.2 0.5 slice_reduce_fusion.33
  3.8 0.1 broadcast_in_dim.1730
  3.9 0.9 broadcast_in_dim.1731.ab
  4.8 1.8 fusion.82
  6.7 1.1 broadcast_compare_fusion.30
  7.8 1.3 select_convert_fusion.5.ay
  9.0 0.5 select_convert_fusion.6
  9.6 0.4 fusion.139
  10.1 0.5 select_convert_fusion.7
  10.6 0.8 pad_maximum_fusion.ax
  11.4 6.3 %fusion.81 = (pred[256,256]{1,0:T(8,128)(4,1)S(1)}, pred[256,256]{1,0:T(8,128)(4,1)S(1)}, pred[256,256]{1,0:T(8,128)(4,1)S(1)}, pred[256,256]{1,0:T(8,128)(4,1)S...) fusion(pred[256,256]{1,0:T(8,128)(4,1)S(1)} %get-tuple-element., ...), kind=kLoop, calls=%fused_computation.127 | loop fusion | flops 6225920 | bytes 5641728 | tf_op jit(solution)/shard_map/eq | solution.py:24
  17.7 2.1 fusion.1.am
  20.0 3.0 %fusion.2 = bf16[3,5,256,256]{3,2,1,0:T(8,128)(2,1)} fusion(bf16[3]{0:T(256)(128)(2,1)} %get-tuple-element.6, bf16[3]{0:T(256)(128)(2,1)} %get-tuple-element.7, bf16[3]{0:T(256)(128)(2,1)} %get-tuple-element.8, bf16[3]{0:T(256)(128)(2,1)} %get-tuple-element.9, bf16[3]{0:T(256)(128)(2,1)} %get-tuple-element.10, bf16[3]{0:T(256)(128)(2,1)} %get-tuple-element.11, ...), kind=kLoop, calls=%fused_computation.30 | loop fusion | flops 3342335 | bytes 1507430
  23.1 2.9 %fusion.3 = bf16[3,5,256,256]{3,2,1,0:T(8,128)(2,1)} fusion(bf16[3,5,256,256]{3,2,1,0:T(8,128)(2,1)} %fusion.2, bf16[3]{0:T(256)(128)(2,1)S(1)} %copy-done.4, bf16[3]{0:T(256)(128)(2,1)S(1)} %copy-done.5, bf16[3]{0:T(256)(128)(2,1)S(1)} %copy-done.6, bf16[3]{0:T(256)(128)(2,1)} %get-tuple-element.9, bf16[3]{0:T(256)(128)(2,1)} %get-tuple-element.10, ...), kind=kLoop, calls=%fused_computation.31 | loop fusion | flops 3342336 | bytes 1514008
  26.1 1.7 fusion.4
  27.8 1.7 fusion.5
  29.5 1.7 fusion.6.az
  31.2 23.3 %relayout_in.1.vin = bf16[4,32,512,128]{3,2,1,0:T(8,128)(2,1)} custom-call(s32[1]{0:T(128)} %bitcast.xi_ref, bf16[32,64,64,64]{3,2,1,0:T(8,128)(2,1)} %x_ref.1), custom_call_target="tpu_custom_call" | custom-call | flops 16777216 | bytes 8388608 | tf_op jit(solution)/shard_map/relayout_in/pallas_call | solution.py:91
  54.4 172.5 %fused_layers.1.v_ref = bf16[4,32,512,128]{3,2,1,0:T(8,128)(2,1)} custom-call(bf16[4,32,512,128]{3,2,1,0:T(8,128)(2,1)} %relayout_in.1.vin, bf16[3,2,128,256]{3,2,1,0:T(8,128)(2,1)} %pad_maximum_fusion.ax, bf16[3,128,256]{2,1,0:T(8,128)(2,1)} %select_convert_fusion.5.ay, bf16[3,5,256,256]{3,2,1,0:T(8,128)(2,1)} %fusion.6.az, bf16[3,256,256]{2,1,0:T(8,128)(2,1)} %fusion.1.am, ...), custom_call_target="tpu_custom_call" | custom-call | flops 4294967296 | bytes 8388608 | tf_op jit(solution)/shard_map/fused_layers/pallas_call | solution.py:406
  226.9 21.1 %relayout_out.1 = bf16[32,64,64,64]{3,2,1,0:T(8,128)(2,1)} custom-call(s32[1]{0:T(128)} %bitcast.xi_ref, bf16[4,32,512,128]{3,2,1,0:T(8,128)(2,1)} %fused_layers.1.v_ref), custom_call_target="tpu_custom_call" | custom-call | flops 67108864 | bytes 8388608 | tf_op jit(solution)/shard_map/relayout_out/pallas_call | solution.py:120
  (72 shorter events, 0.4 us)
Async XLA Ops:
  0.0 9.6 %copy-start.25 = (pred[256]{0:T(512)(128)(4,1)}, pred[256]{0:T(512)(128)(4,1)S(1)}, u32[]{:S(2)}) copy-start(pred[256]{0:T(512)(128)(4,1)S(1)} %fusion.169) | copy-start | bytes 772
  0.1 9.5 %copy-start.23 = (pred[256]{0:T(512)(128)(4,1)}, pred[256]{0:T(512)(128)(4,1)S(1)}, u32[]{:S(2)}) copy-start(pred[256]{0:T(512)(128)(4,1)S(1)} %get-tuple-element.282) | copy-start | bytes 772
  0.1 9.5 %copy-start.24 = (pred[256]{0:T(512)(128)(4,1)}, pred[256]{0:T(512)(128)(4,1)S(1)}, u32[]{:S(2)}) copy-start(pred[256]{0:T(512)(128)(4,1)S(1)} %get-tuple-element.295) | copy-start | bytes 772
  0.8 8.8 %copy-start.20 = (s32[256]{0:T(256)}, s32[256]{0:T(256)S(1)}, u32[]{:S(2)}) copy-start(s32[256]{0:T(256)S(1)} %get-tuple-element.291) | copy-start | bytes 3076
  0.9 8.7 %copy-start.22 = (s32[256]{0:T(256)}, s32[256]{0:T(256)S(1)}, u32[]{:S(2)}) copy-start(s32[256]{0:T(256)S(1)} %get-tuple-element.296) | copy-start | bytes 3076
  0.9 8.7 %copy-start.21 = (s32[256]{0:T(256)}, s32[256]{0:T(256)S(1)}, u32[]{:S(2)}) copy-start(s32[256]{0:T(256)S(1)} %get-tuple-element.278) | copy-start | bytes 3076
  17.7 5.3 %copy-start.3 = (bf16[3]{0:T(256)(128)(2,1)S(1)}, bf16[3]{0:T(256)(128)(2,1)}, u32[]{:S(2)}) copy-start(bf16[3]{0:T(256)(128)(2,1)} %get-tuple-element.5) | copy-start | bytes 22
  17.7 5.3 %copy-start.4 = (bf16[3]{0:T(256)(128)(2,1)S(1)}, bf16[3]{0:T(256)(128)(2,1)}, u32[]{:S(2)}) copy-start(bf16[3]{0:T(256)(128)(2,1)} %get-tuple-element.6) | copy-start | bytes 22
  19.8 6.2 %copy-start.2 = (pred[256,256]{1,0:T(8,128)(4,1)S(1)}, pred[256,256]{1,0:T(8,128)(4,1)}, u32[]{:S(2)}) copy-start(pred[256,256]{1,0:T(8,128)(4,1)} %get-tuple-element.166) | copy-start | bytes 196612
  19.8 6.2 %copy-start.7 = (bf16[3]{0:T(256)(128)(2,1)S(1)}, bf16[3]{0:T(256)(128)(2,1)}, u32[]{:S(2)}) copy-start(bf16[3]{0:T(256)(128)(2,1)} %get-tuple-element.9) | copy-start | bytes 22
  19.8 6.2 %copy-start.8 = (bf16[3]{0:T(256)(128)(2,1)S(1)}, bf16[3]{0:T(256)(128)(2,1)}, u32[]{:S(2)}) copy-start(bf16[3]{0:T(256)(128)(2,1)} %get-tuple-element.10) | copy-start | bytes 22
  19.8 6.2 %copy-start.9 = (bf16[3]{0:T(256)(128)(2,1)S(1)}, bf16[3]{0:T(256)(128)(2,1)}, u32[]{:S(2)}) copy-start(bf16[3]{0:T(256)(128)(2,1)} %get-tuple-element.11) | copy-start | bytes 22
  19.9 6.2 %copy-start.10 = (bf16[3]{0:T(256)(128)(2,1)S(1)}, bf16[3]{0:T(256)(128)(2,1)}, u32[]{:S(2)}) copy-start(bf16[3]{0:T(256)(128)(2,1)} %get-tuple-element.12) | copy-start | bytes 22
  19.9 6.2 %copy-start.11 = (bf16[3]{0:T(256)(128)(2,1)S(1)}, bf16[3]{0:T(256)(128)(2,1)}, u32[]{:S(2)}) copy-start(bf16[3]{0:T(256)(128)(2,1)} %get-tuple-element.13) | copy-start | bytes 22
  19.9 6.2 %copy-start.12 = (bf16[3]{0:T(256)(128)(2,1)S(1)}, bf16[3]{0:T(256)(128)(2,1)}, u32[]{:S(2)}) copy-start(bf16[3]{0:T(256)(128)(2,1)} %get-tuple-element.14) | copy-start | bytes 22
  19.9 6.2 %copy-start.13 = (bf16[3]{0:T(256)(128)(2,1)S(1)}, bf16[3]{0:T(256)(128)(2,1)}, u32[]{:S(2)}) copy-start(bf16[3]{0:T(256)(128)(2,1)} %get-tuple-element.15) | copy-start | bytes 22
  19.9 6.2 %copy-start.14 = (bf16[3]{0:T(256)(128)(2,1)S(1)}, bf16[3]{0:T(256)(128)(2,1)}, u32[]{:S(2)}) copy-start(bf16[3]{0:T(256)(128)(2,1)} %get-tuple-element.16) | copy-start | bytes 22
  19.9 6.2 %copy-start.15 = (bf16[3]{0:T(256)(128)(2,1)S(1)}, bf16[3]{0:T(256)(128)(2,1)}, u32[]{:S(2)}) copy-start(bf16[3]{0:T(256)(128)(2,1)} %get-tuple-element.17) | copy-start | bytes 22
  19.9 6.2 %copy-start.16 = (bf16[3]{0:T(256)(128)(2,1)S(1)}, bf16[3]{0:T(256)(128)(2,1)}, u32[]{:S(2)}) copy-start(bf16[3]{0:T(256)(128)(2,1)} %get-tuple-element.18) | copy-start | bytes 22
  19.9 6.2 %copy-start.17 = (bf16[3]{0:T(256)(128)(2,1)S(1)}, bf16[3]{0:T(256)(128)(2,1)}, u32[]{:S(2)}) copy-start(bf16[3]{0:T(256)(128)(2,1)} %get-tuple-element.19) | copy-start | bytes 22
  19.9 6.2 %copy-start.18 = (bf16[3]{0:T(256)(128)(2,1)S(1)}, bf16[3]{0:T(256)(128)(2,1)}, u32[]{:S(2)}) copy-start(bf16[3]{0:T(256)(128)(2,1)} %get-tuple-element.20) | copy-start | bytes 22
  19.9 6.2 %copy-start.19 = (bf16[3]{0:T(256)(128)(2,1)S(1)}, bf16[3]{0:T(256)(128)(2,1)}, u32[]{:S(2)}) copy-start(bf16[3]{0:T(256)(128)(2,1)} %get-tuple-element.21) | copy-start | bytes 22
  20.0 7.9 %copy-start.1 = (pred[256,256]{1,0:T(8,128)(4,1)S(1)}, pred[256,256]{1,0:T(8,128)(4,1)}, u32[]{:S(2)}) copy-start(pred[256,256]{1,0:T(8,128)(4,1)} %get-tuple-element.164) | copy-start | bytes 196612
  23.1 6.4 %copy-start = (pred[256,256]{1,0:T(8,128)(4,1)S(1)}, pred[256,256]{1,0:T(8,128)(4,1)}, u32[]{:S(2)}) copy-start(pred[256,256]{1,0:T(8,128)(4,1)} %get-tuple-element.56) | copy-start | bytes 196612
  (2 other events, 10.7 us)

commit v3 on v2

--- a/solution.py
+++ b/solution.py
@@ -17,51 +17,78 @@
     return lax.broadcasted_iota(jnp.int32, shape, len(shape) - 1)
 
 
-def pick_taps(index, valid, taps):
+def iota2(rows, cols, row0=0):
+    return lax.broadcasted_iota(jnp.int32, (rows, cols), 0) + row0, lax.broadcasted_iota(jnp.int32, (rows, cols), 1)
+
+
+def tap_values(taps, row, index, valid, mirrored=None):
     index = jnp.where(valid, index, -1)
-    out = jnp.zeros((taps.shape[0],) + index.shape, F32)
-    for t in range(taps.shape[1]):
-        out = jnp.where(index[None] == t, taps[:, t][:, None, None], out)
-    return out.astype(BF)
-
-
-def grid2(rows, cols):
-    return (lax.broadcasted_iota(jnp.int32, (rows, cols), 0), lax.broadcasted_iota(jnp.int32, (rows, cols), 1))
-
-
-def x_table(taps, last):
-    r, q = grid2(128, 256)
-    i_out, i_in = r // 8, q // 8
-    if last:
-        i_in = jnp.where(i_in >= 24, 55 - i_in, i_in)
-    t = i_in - i_out
-    return pick_taps(t, (t >= 0) & (t <= 16) & (r % 8 == q % 8), taps)
-
-
-def y_table(taps):
-    r, q = grid2(128, 256)
-    t = (q // 64) * 8 + q % 8 - (r // 64) * 8 - r % 8
-    return pick_taps(t, (t >= 0) & (t <= 16) & ((r // 8) % 8 == (q // 8) % 8), taps)
-
-
-def z_tables(taps):
-    m, n = grid2(256, 256)
-    t = m % 64 - n % 64 + 8
-    tables = [pick_taps(t, (t >= 0) & (t <= 16) & (m // 64 == n // 64), taps)]
-    for v in range(4):
-        k = jnp.where(m < 128, -8, 64) + m % 8
-        t = k - n % 64 + 8
-        ok = ((m // 64) % 2 == (n // 64) % 2) & ((m // 8) % 8 == 2 * v + n // 128)
-        tables.append(pick_taps(t, (t >= 0) & (t <= 16) & ok, taps))
-    return jnp.stack(tables, axis=1)
-
-
-def mix_table(mix_w):
-    r, q = grid2(256, 32)
-    spread = (r // 8 == q).astype(BF)
-    full = jnp.einsum("rd,lcd,qc->lrq", spread, mix_w, spread, preferred_element_type=F32)
-    r, q = grid2(256, 256)
-    return jnp.where((r % 8 == q % 8)[None], 0.5 * full, 0.0).astype(BF)
+    count = taps.shape[1]
+    out = jnp.zeros(index.shape, F32)
+    for t in range(count):
+        src = t if mirrored is None else jnp.where(mirrored, count - 1 - t, t)
+        out = jnp.where(index == t, taps[row, src], out)
+    return out
+
+
+def build_x_tables(taps, ax, mirrored):
+    span = taps.shape[1]
+
+    def layer(l, _):
+        for last in range(2):
+            for r0 in range(0, 128, 32):
+                r, q = iota2(32, 256, r0)
+                i_in = q // 8
+                if last:
+                    i_in = jnp.where(i_in >= 24, 55 - i_in, i_in)
+                t = i_in - r // 8
+                ok = (t >= 0) & (t < span) & (r % 8 == q % 8)
+                ax[l, last, r0 : r0 + 32, :] = tap_values(taps, 3 * l, t, ok, mirrored).astype(BF)
+        return 0
+
+    lax.fori_loop(0, ax.shape[0], layer, 0)
+
+
+def build_tables(taps, mix_w, bias, ay, az, am, ab):
+    C = mix_w.shape[1]
+    span = taps.shape[1]
+
+    def layer(l, _):
+        for r0 in range(0, 128, 32):
+            r, q = iota2(32, 256, r0)
+            t = (q // 64) * 8 + q % 8 - (r // 64) * 8 - r % 8
+            ok = (t >= 0) & (t < span) & ((r // 8) % 8 == (q // 8) % 8)
+            ay[l, r0 : r0 + 32, :] = tap_values(taps, 3 * l + 1, t, ok).astype(BF)
+        for k0 in range(0, 64, 32):
+            k, n = iota2(32, 256, k0)
+            t = k - n % 64 + 8
+            base = tap_values(taps, 3 * l + 2, t, (t >= 0) & (t < span))
+            for g in range(4):
+                az[l, 0, 64 * g + k0 : 64 * g + k0 + 32, :] = jnp.where(n // 64 == g, base, 0.0).astype(BF)
+        for v in range(4):
+            for r0 in range(0, 256, 64):
+                az[l, 1 + v, r0 : r0 + 64, :] = jnp.zeros((64, 256), BF)
+        r, n = iota2(16, 256)
+        for side in range(2):
+            t = r % 8 - n % 64 + 72 * side
+            base = tap_values(taps, 3 * l + 2, t, (t >= 0) & (t < span) & (r // 8 == n // 128))
+            for jh in range(2):
+                block = jnp.where((n // 64) % 2 == jh, base, 0.0).astype(BF)
+                for v in range(4):
+                    r0 = 128 * side + 64 * jh + 16 * v
+                    az[l, 1 + v, r0 : r0 + 16, :] = block
+        r, q = iota2(8 * C, C)
+        spread = jnp.where(r // 8 == q, 1.0, 0.0).astype(BF)
+        nt = (((1,), (1,)), ((), ()))
+        half = lax.dot_general(spread, mix_w[l], nt, preferred_element_type=F32).astype(BF)
+        full = lax.dot_general(half, spread, nt, preferred_element_type=F32)
+        r, q = iota2(8 * C, 8 * C)
+        am[l] = jnp.where(r % 8 == q % 8, 0.5 * full, 0.0).astype(BF)
+        for d in range(C):
+            ab[l, 8 * d : 8 * d + 8, :] = jnp.full((8, 128), 0.5 * bias[l, d], F32)
+        return 0
+
+    lax.fori_loop(0, ay.shape[0], layer, 0)
 
 
 def cost(flops):
@@ -72,40 +99,9 @@
     return pltpu.CompilerParams(vmem_limit_bytes=60 << 20)
 
 
-def relayout_in(volume, xi):
-    C, I, J, K = volume.shape
-    n_slab, cb = I // SLAB, 8
-
-    def body(xi_ref, x_ref, o_ref):
-        flip = xi_ref[0]
-        for tp in range(SLAB // 2):
-            rows = []
-            for t in (2 * tp, 2 * tp + 1):
-                a = x_ref[:, jnp.where(flip == 1, SLAB - 1 - t, t)].astype(F32)
-                a = jnp.concatenate([a[:, : J // 2], a[:, J // 2 :]], axis=2)
-                rows.append(a.reshape(cb, 4, 8, 128))
-            both = jnp.concatenate(rows, axis=2).astype(BF)
-            for jb in range(4):
-                o_ref[jb, :, 16 * tp : 16 * tp + 16, :] = both[:, jb]
-
-    return pl.pallas_call(
-        body,
-        grid_spec=pltpu.PrefetchScalarGridSpec(
-            num_scalar_prefetch=1,
-            grid=(n_slab, C // cb),
-            in_specs=[pl.BlockSpec((cb, SLAB, J, K), lambda s, g, f: (g, jnp.where(f[0] == 1, n_slab - 1 - s, s), 0, 0))],
-            out_specs=pl.BlockSpec((4, cb, SLAB * 8, 128), lambda s, g, f: (0, g, s, 0)),
-        ),
-        out_shape=jax.ShapeDtypeStruct((4, C, I * 8, 128), BF),
-        compiler_params=params(),
-        cost_estimate=cost(1 << 24),
-        name="relayout_in",
-    )(xi, volume)
-
-
 def relayout_out(vol, xi, shape):
     C, I, J, K = shape
-    cb = 2
+    cb = 4
 
     def body(xi_ref, v_ref, o_ref):
         flip = xi_ref[0]
@@ -235,15 +231,17 @@
     lax.fori_loop(0, 4, step, 0)
 
 
-def fused_layers(v_in, xt, yt, zt, mt, bt, ny, nz):
-    C, rows = v_in.shape[1], v_in.shape[2]
-    L = xt.shape[0]
+def fused_layers(volume, filter_taps, mix_w, mix_bias, ny, nz):
+    C, I, J, K = volume.shape
+    rows = 8 * I
+    L = mix_w.shape[0]
+    IN = 4
     S = rows // 128
     N = L * S
     R = 4
     edge = 64 + rows
 
-    def body(vin, ax, ay, az, am, ab, vout, vol, far, u1, u2, u3, ysend, yrecv, zsend, zrecv,
+    def body(vin, taps, wraw, braw, vout, ax, ay, az, am, ab, stage_in, vol, far, u1, u2, u3, ysend, yrecv, zsend, zrecv,
              in_sem, out_sem, far_ss, far_rs, ys_sem, yr_sem, zs_sem, zr_sem):
         xi, yi, zi = (lax.axis_index(a) for a in ("x", "y", "z"))
 
@@ -289,15 +287,43 @@
             a = l % 2
             return remote(vol.at[:, :, pl.ds(edge - 64, 64), :], far.at[a], far_ss.at[a], far_rs.at[a], "x", 1 - xi)
 
-        def in_copy(s):
-            return pltpu.make_async_copy(vin.at[:, :, pl.ds(128 * s, 128), :], vol.at[:, :, pl.ds(64 + 128 * s, 128), :], in_sem.at[s])
+        mirrored = xi == 1
+
+        def in_copy(q):
+            at = jnp.where(mirrored, I - 2 - 2 * q, 2 * q)
+            return pltpu.make_async_copy(vin.at[:, pl.ds(at, 2)], stage_in.at[q % IN], in_sem.at[q % IN])
+
+        def bring_in(q, _):
+            in_copy(q).wait()
+            per = 16
+
+            def part(g, _):
+                c = pl.ds(per * g, per)
+                planes = []
+                for u in range(2):
+                    a = stage_in[q % IN, c, jnp.where(mirrored, 1 - u, u)].astype(F32)
+                    a = jnp.concatenate([a[:, : J // 2], a[:, J // 2 :]], axis=2)
+                    planes.append(a.reshape(per, 4, 8, 128))
+                both = jnp.concatenate(planes, axis=2).astype(BF)
+                at = pl.ds(pl.multiple_of(64 + 16 * q, 16), 16)
+                for jb in range(4):
+                    vol[jb, c, at, :] = both[:, jb]
+                return 0
+
+            lax.fori_loop(0, C // per, part, 0)
+
+            @pl.when(q + IN < I // 2)
+            def _():
+                in_copy(q + IN).start()
+
+            return 0
 
         def out_copy(s):
             at = pl.multiple_of(128 * s, 128)
             return pltpu.make_async_copy(vol.at[:, :, pl.ds(64 + at, 128), :], vout.at[:, :, pl.ds(at, 128), :], out_sem.at[s])
 
-        for s in range(S):
-            in_copy(s).start()
+        for q in range(IN):
+            in_copy(q).start()
         barrier = pltpu.get_barrier_semaphore()
         pl.semaphore_signal(barrier, inc=1, device_id={"x": 1 - xi}, device_id_type=pl.DeviceIdType.MESH)
         for axis, pos, count in (("y", yi, ny), ("z", zi, nz)):
@@ -316,16 +342,20 @@
             return 0
 
         lax.fori_loop(0, C, zero_margin, 0)
-        for recv, pos, count in ((yrecv, yi, ny), (zrecv, zi, nz)):
-            for d, alone in ((0, pos == 0), (1, pos == count - 1)):
-                @pl.when(alone)
-                def _():
-                    def zero(r, _):
-                        for j in range(recv.shape[2]):
-                            recv[d, r, j] = jnp.zeros(recv.shape[3:], BF)
-                        return 0
-
-                    lax.fori_loop(0, R, zero, 0)
+        build_x_tables(taps, ax, mirrored)
+
+        def late_setup():
+            for recv, pos, count in ((yrecv, yi, ny), (zrecv, zi, nz)):
+                for d, alone in ((0, pos == 0), (1, pos == count - 1)):
+                    @pl.when(alone)
+                    def _():
+                        def zero(r, _):
+                            for j in range(recv.shape[2]):
+                                recv[d, r, j] = jnp.zeros(recv.shape[3:], BF)
+                            return 0
+
+                        lax.fori_loop(0, R, zero, 0)
+            build_tables(taps, wraw, braw, ay, az, am, ab)
 
         def stage(n, _):
             @pl.when(n < N)
@@ -334,14 +364,13 @@
 
                 @pl.when(n == 0)
                 def _():
-                    in_copy(0).wait()
-                    in_copy(1).wait()
+                    lax.fori_loop(0, 3 * SLAB // 4, bring_in, 0)
 
                 @pl.when(n == 1)
                 def _():
-                    for q in range(2, S):
-                        in_copy(q).wait()
+                    lax.fori_loop(3 * SLAB // 4, I // 2, bring_in, 0)
                     far_copy(0).start()
+                    late_setup()
 
                 @pl.when(s == S - 1)
                 def _():
@@ -401,14 +430,21 @@
             out_copy(s).wait()
 
     vmem = pl.BlockSpec(memory_space=pltpu.VMEM)
+    smem = pl.BlockSpec(memory_space=pltpu.SMEM)
     hbm = pl.BlockSpec(memory_space=pltpu.HBM)
     dma = pltpu.SemaphoreType.DMA
     return pl.pallas_call(
         body,
-        in_specs=[hbm] + [vmem] * 5,
+        in_specs=[hbm, smem, vmem, smem],
         out_specs=hbm,
-        out_shape=jax.ShapeDtypeStruct(v_in.shape, BF),
+        out_shape=jax.ShapeDtypeStruct((4, C, rows, 128), BF),
         scratch_shapes=[
+            pltpu.VMEM((L, 2, 128, 256), BF),
+            pltpu.VMEM((L, 128, 256), BF),
+            pltpu.VMEM((L, 5, 256, 256), BF),
+            pltpu.VMEM((L, 8 * C, 8 * C), BF),
+            pltpu.VMEM((L, 8 * C, 128), F32),
+            pltpu.VMEM((IN, C, 2, J, K), BF),
             pltpu.VMEM((4, C, rows + 128, 128), BF),
             pltpu.VMEM((2, 4, C, 64, 128), BF),
             pltpu.VMEM((2, C, 4, 128, 128), BF),
@@ -418,7 +454,7 @@
             pltpu.VMEM((2, R, C // 2, 128, 128), BF),
             pltpu.VMEM((2, 2, 4, 2, 8 * C, 128), BF),
             pltpu.VMEM((2, R, 4, 2, 8 * C, 128), BF),
-            dma((S,)),
+            dma((IN,)),
             dma((S,)),
             dma((2,)),
             dma((2,)),
@@ -430,7 +466,7 @@
         compiler_params=pltpu.CompilerParams(vmem_limit_bytes=67043328, collective_id=0, has_side_effects=True),
         cost_estimate=cost(1 << 32),
         name="fused_layers",
-    )(v_in, xt, yt, zt, mt, bt)
+    )(volume, filter_taps.reshape(-1, filter_taps.shape[2]), mix_w, mix_bias)
 
 
 def solution(mesh):
@@ -439,13 +475,7 @@
     def local_layers(volume, filter_taps, mix_w, mix_bias):
         xi = lax.axis_index("x").astype(jnp.int32)
         xi_arr = xi.reshape(1)
-        layers = filter_taps.shape[0]
-        taps = filter_taps.astype(BF).astype(F32)
-        taps_x = jnp.where(xi == 1, taps[:, 0, ::-1], taps[:, 0])
-        xt = jnp.stack([x_table(taps_x, False), x_table(taps_x, True)], axis=1)
-        yt, zt, mt = y_table(taps[:, 1]), z_tables(taps[:, 2]), mix_table(mix_w)
-        bt = jnp.broadcast_to(jnp.repeat(0.5 * mix_bias, 8, axis=1)[:, :, None], (layers, 256, 128))
-        out = fused_layers(relayout_in(volume, xi_arr), xt, yt, zt, mt, bt, ny, nz)
+        out = fused_layers(volume, filter_taps, mix_w, mix_bias, ny, nz)
         return relayout_out(out, xi_arr, volume.shape)
 
     vol_spec = P("batch", "x", "y", "z")

time: 249 us -> 197 us (0.79)
  other arithmetic: 25.3 us -> 0 us
  Pallas kernels: 217 us -> 195 us
    pallas_call x2 -> x1, Pallas kernels: 196 us -> 176 us  [fused_layers(): pl.pallas_call(body, in_specs=[hbm, smem, vmem, smem], out_specs=hbm, out...]
    eq x4 -> x0, other arithmetic: 9.71 us -> none  [pick_taps(): out = jnp.where(index[None] == t, taps[:, t][:, None, None], out)]
    unnamed x4 -> x0, other arithmetic: 9.34 us -> none
    convert_element_type x4 -> x0, other arithmetic: 2.99 us -> none  [the longest x3 2.3 us: pick_taps(): return out.astype(BF)]
where the time goes in v3:
time: 197 us
  Pallas kernels  195 us (99%)
    pallas_call x1, Pallas kernels, fused_layers(): pl.pallas_call(body, in_specs=[hbm, smem, vmem, smem], out_specs=hbm, out...  176 us
    pallas_call x1, Pallas kernels, relayout_out(): pl.pallas_call(body, grid_spec=pltpu.PrefetchScalarGridSpec(num_scalar_pr...  19.2 us

profile of v3, /device:TPU:98, one launch (start us, length us, event | category | flops | bytes accessed | tf_op | source)
XLA Modules:
  0.0 196.5 jit_solution(10358463741987495856)
XLA Ops:
  0.0 1.3 reshape.7.taps
  1.3 176.0 %fused_layers.1.v_ref = bf16[4,32,512,128]{3,2,1,0:T(8,128)(2,1)} custom-call(bf16[32,64,64,64]{3,2,1,0:T(8,128)(2,1)} %vin.1, f32[9,17]{1,0:T(8,128)} %reshape.7.taps, bf16[3,32,32]{2,1,0:T(8,128)(2,1)} %wraw.1, f32[3,32]{1,0:T(4,128)} %braw.1), custom_call_target="tpu_custom_call" | custom-call | flops 4294967296 | bytes 8388608 | tf_op jit(solution)/shard_map/fused_layers/pallas_call | solution.py:436
  177.3 19.2 %relayout_out.1 = bf16[32,64,64,64]{3,2,1,0:T(8,128)(2,1)} custom-call(s32[1]{0:T(128)} %bitcast.xi_ref, bf16[4,32,512,128]{3,2,1,0:T(8,128)(2,1)} %fused_layers.1.v_ref), custom_call_target="tpu_custom_call" | custom-call | flops 67108864 | bytes 8388608 | tf_op jit(solution)/shard_map/relayout_out/pallas_call | solution.py:116

commit v4 on v3

--- a/solution.py
+++ b/solution.py
@@ -8,7 +8,8 @@
 BF = jnp.bfloat16
 F32 = jnp.float32
 SLAB = 16
-X_UNROLL, Y_UNROLL = 8, 4
+X_UNROLL, Y_UNROLL = 16, 4
+Z_UNROLL, Z_AHEAD = 2, 2
 JH = 2
 SQRT_TWO = 1.4142135623730951
 
@@ -211,24 +212,26 @@
         u3 = u3 + jnp.dot(halo, z_ref[1 + ip % 4], preferred_element_type=F32)
         return u3.astype(BF)
 
-    u3_ref[...] = z_pair(0, 0)
-
-    def step(jb, _):
-        u3 = u3_ref[...]
-        for ip in range(8):
-            ahead = z_pair(jb, ip + 1) if ip < 7 else z_pair(jnp.minimum(jb + 1, 3), 0)
+    for q in range(Z_AHEAD):
+        u3_ref[q] = z_pair(0, q)
+
+    def step(it, _):
+        u3 = [u3_ref[q] for q in range(Z_AHEAD)]
+        for q in range(8 * Z_UNROLL):
+            jb, ip, nxt = it * Z_UNROLL + q // 8, q % 8, q % 8 + Z_AHEAD
+            u3.append(z_pair(jnp.minimum(jb + nxt // 8, 3), nxt % 8))
             bias = bias_ref[...].reshape(C, 8, 128)
-            m = jnp.dot(w_ref[...], u3, preferred_element_type=F32).reshape(C, 8, 256)
+            m = jnp.dot(w_ref[...], u3[q], preferred_element_type=F32).reshape(C, 8, 256)
             m = jnp.concatenate([m[..., :128] + bias, m[..., 128:] + bias], axis=1)
             gelu = m + m * lax.erf(m * SQRT_TWO)
             rows = pl.ds(pl.multiple_of(row0 + 16 * ip, 16), 16)
             v = vol[jb, :, rows, :].astype(F32)
             vol[jb, :, rows, :] = (v + gelu).astype(BF)
-            u3 = ahead
-        u3_ref[...] = u3
+        for q in range(Z_AHEAD):
+            u3_ref[q] = u3[8 * Z_UNROLL + q]
         return 0
 
-    lax.fori_loop(0, 4, step, 0)
+    lax.fori_loop(0, 4 // Z_UNROLL, step, 0)
 
 
 def fused_layers(volume, filter_taps, mix_w, mix_bias, ny, nz):
@@ -449,7 +452,7 @@
             pltpu.VMEM((2, 4, C, 64, 128), BF),
             pltpu.VMEM((2, C, 4, 128, 128), BF),
             pltpu.VMEM((2, 4, SLAB, 8 * C, 128), BF),
-            pltpu.VMEM((8 * C, 256), BF),
+            pltpu.VMEM((Z_AHEAD, 8 * C, 256), BF),
             pltpu.VMEM((2, 2, C // 2, 128, 128), BF),
             pltpu.VMEM((2, R, C // 2, 128, 128), BF),
             pltpu.VMEM((2, 2, 4, 2, 8 * C, 128), BF),

time: 197 us -> 192 us (0.975)
  Pallas kernels: 195 us -> 190 us
    pallas_call x1, Pallas kernels: 176 us -> 171 us  [fused_layers(): pl.pallas_call(body, in_specs=[hbm, smem, vmem, smem], out_specs=hbm, out...]
where the time goes in v4:
time: 192 us
  Pallas kernels  190 us (99%)
    pallas_call x1, Pallas kernels, fused_layers(): pl.pallas_call(body, in_specs=[hbm, smem, vmem, smem], out_specs=hbm, out...  171 us
    pallas_call x1, Pallas kernels, relayout_out(): pl.pallas_call(body, grid_spec=pltpu.PrefetchScalarGridSpec(num_scalar_pr...  19.2 us

profile of v4, /device:TPU:98, one launch (start us, length us, event | category | flops | bytes accessed | tf_op | source)
XLA Modules:
  0.0 191.8 jit_solution(4240931772015388359)
XLA Ops:
  0.0 1.3 reshape.7.taps
  1.3 171.3 %fused_layers.1.v_ref = bf16[4,32,512,128]{3,2,1,0:T(8,128)(2,1)} custom-call(bf16[32,64,64,64]{3,2,1,0:T(8,128)(2,1)} %vin.1, f32[9,17]{1,0:T(8,128)} %reshape.7.taps, bf16[3,32,32]{2,1,0:T(8,128)(2,1)} %wraw.1, f32[3,32]{1,0:T(4,128)} %braw.1), custom_call_target="tpu_custom_call" | custom-call | flops 4294967296 | bytes 8388608 | tf_op jit(solution)/shard_map/fused_layers/pallas_call | solution.py:439
  172.6 19.2 %relayout_out.1 = bf16[32,64,64,64]{3,2,1,0:T(8,128)(2,1)} custom-call(s32[1]{0:T(128)} %bitcast.xi_ref, bf16[4,32,512,128]{3,2,1,0:T(8,128)(2,1)} %fused_layers.1.v_ref), custom_call_target="tpu_custom_call" | custom-call | flops 67108864 | bytes 8388608 | tf_op jit(solution)/shard_map/relayout_out/pallas_call | solution.py:117
